TPU v7x, 256 devices: a whole 4x4x8 slice. The times are simulated.
256 devices in a mesh: sx: 8 (over y, core), sy: 4 (over x), sz: 8 (over z).
Axes of the slice: x: 4, y: 4, z: 8, core: 2. Of those that a mesh axis runs over, the one named last changes fastest.
Arguments:
- right_side: bfloat16 [8, 4, 8, 1536, 256], P('sx', 'sy', 'sz'), may hold values from -6 to 6
- interface_inverse: bfloat16 [8, 4, 8, 1536, 1536], P('sx', 'sy', 'sz'), may hold values from -2 to 2, as said below
- face_link: int32 [8, 4, 8, 4], P('sx', 'sy', 'sz'), may hold values 0 or 1
- far_target: int32 [8, 4, 8, 64, 1], P('sx', 'sy', 'sz'), may hold values from 0 to 63; in each aligned block of 64 rows (0 to 63, 64 to 127, ..., all dimensions but the last counted through in order) at most 3 rows name the same one
- far_rank: int32 [8, 4, 8, 64], P('sx', 'sy', 'sz'), may hold values from 1 to 16
- far_basis: bfloat16 [8, 4, 8, 64, 16, 1536], P('sx', 'sy', 'sz'), may hold values from -0.15625 to 0.15625
- patch_basis: bfloat16 [8, 4, 8, 16, 1536], P('sx', 'sy', 'sz'), may hold values from -0.1875 to 0.1875
- corner_basis: bfloat16 [8, 4, 8, 8, 1536], P('sx', 'sy', 'sz'), may hold values from -1 to 1
- corner_row: int32 [8, 4, 8, 8], P('sx', 'sy', 'sz'), may hold values from 0 to 2047
- coarse_inverse: bfloat16 [2048, 2048], P('sy'), may hold values from -2 to 2, as said below
Outputs:
- multipliers: float32 [8, 4, 8, 1536, 256], P('sx', 'sy', 'sz')
- interface_field: bfloat16 [8, 4, 8, 1536, 256], P('sx', 'sy', 'sz')
Inputs may be any that keep to these rules, and one draw needn't show every extreme that they name: `far_target`: within one subdomain's 64 entries no target is named more than 3 times, a bound that some block reaches. `interface_inverse`: each subdomain's block is a dense matrix with a positive diagonal that exceeds its row's off-diagonal magnitude in the root-mean-square sense. `coarse_inverse`: A dense matrix with a positive diagonal that exceeds its row's off-diagonal magnitude in the root-mean-square sense.
All inputs are finite; a program needn't handle non-finite values. No bound on the sum of `face_link` on one device may be relied on, other than what follows from the above.
Results may differ from a plain program's by a relative error of at most 0.0085.
Values may be sent and summed in bfloat16 or wider, within the bound.
No kernel may reach another device: no remote copies, remote signals or barrier semaphores. Data moves between devices by JAX's collectives and lax.ppermute only.
A program may use at most 64 MiB of HBM per device.

v0:
```python
import jax
import jax.numpy as jnp
from jax import lax
from jax.sharding import PartitionSpec as P

MOST = 3
ITERS = 2


def shifted(block, axis, distance):
    devices = range(lax.axis_size(axis))
    route = [(i - distance, i) for i in devices if i - distance in devices]
    return lax.ppermute(block, axis, route)


def neighbour_faces(solved, face_rows, link_weights, padding):
    pieces = []
    for offset, sent_face in ((1, 1), (-1, 0)):
        outgoing = solved[sent_face * face_rows : (sent_face + 1) * face_rows]
        pieces.append(shifted(outgoing, "sx", offset))
    for offset, sent_face in ((1, 3), (-1, 2)):
        outgoing = solved[sent_face * face_rows : (sent_face + 1) * face_rows]
        pieces.append(shifted(outgoing, "sy", offset))
    scaled = [pieces[number].astype(jnp.float32) * link_weights[number] for number in range(4)]
    return jnp.concatenate(scaled + [padding], axis=0)


def body(
    right_side,
    interface_inverse,
    face_link,
    far_target,
    far_rank,
    far_basis,
    patch_basis,
    corner_basis,
    corner_row,
    coarse_inverse,
):
    order_size = interface_inverse.shape[-1]
    columns = right_side.shape[-1]
    face_rows = order_size // 6
    inverse = interface_inverse.reshape(order_size, order_size)
    source = right_side.reshape(order_size, columns).astype(jnp.float32)
    link_weights = face_link.reshape(4).astype(jnp.float32)
    targets = far_target.reshape(-1)
    entries = targets.shape[0]
    rank_limit = far_basis.shape[-2]
    bases = far_basis.reshape(entries * rank_limit, order_size)
    kept_rows = (
        jnp.arange(rank_limit, dtype=jnp.int32)[None, :] < far_rank.reshape(entries, 1)
    ).astype(jnp.float32)
    patch = patch_basis.reshape(rank_limit, order_size)
    corners = corner_basis.reshape(-1, order_size)
    corner_ids = corner_row.reshape(-1)
    coarse_order = coarse_inverse.shape[1]
    group_size = lax.axis_size("sx") * lax.axis_size("sz")
    corner_hot = (corner_ids[None, :] == jnp.arange(coarse_order, dtype=jnp.int32)[:, None]).astype(
        jnp.float32
    )
    pick_table = corner_hot.T.astype(jnp.bfloat16)
    padding = jnp.zeros((order_size - 4 * face_rows, columns), jnp.float32)
    earlier = (
        jnp.arange(entries, dtype=jnp.int32)[:, None]
        > jnp.arange(entries, dtype=jnp.int32)[None, :]
    )
    same_target = targets[:, None] == targets[None, :]
    slot_number = jnp.sum(jnp.logical_and(earlier, same_target).astype(jnp.int32), axis=1)
    slot_key = targets * MOST + slot_number
    route_table = (
        slot_key[None, :] == jnp.arange(group_size * MOST, dtype=jnp.int32)[:, None]
    ).astype(jnp.bfloat16)
    multipliers = source
    for sweep in range(ITERS):
        solved = jnp.dot(
            inverse, multipliers.astype(jnp.bfloat16), preferred_element_type=jnp.float32
        ).astype(jnp.bfloat16)
        neighbour = neighbour_faces(solved, face_rows, link_weights, padding)
        coefficient = jnp.dot(bases, solved, preferred_element_type=jnp.float32).reshape(
            entries, rank_limit, columns
        )
        coefficient = (
            (coefficient * kept_rows[:, :, None])
            .astype(jnp.bfloat16)
            .reshape(entries, rank_limit * columns)
        )
        routed = jnp.dot(route_table, coefficient, preferred_element_type=jnp.float32)
        outgoing = routed.astype(jnp.bfloat16).reshape(group_size, MOST, rank_limit, columns)
        arrived_slots = lax.all_to_all(
            outgoing, ("sx", "sz"), split_axis=0, concat_axis=0, tiled=True
        )
        arrived = jnp.sum(arrived_slots.astype(jnp.float32), axis=(0, 1))
        far_term = lax.dot_general(
            patch,
            arrived.astype(jnp.bfloat16),
            (((0,), (0,)), ((), ())),
            preferred_element_type=jnp.float32,
        )
        corner_terms = jnp.dot(corners, solved, preferred_element_type=jnp.float32)
        partial_sum = jnp.dot(corner_hot, corner_terms, precision=lax.Precision.HIGHEST)
        coarse_sum = lax.psum(partial_sum, ("sx", "sy", "sz")).astype(jnp.bfloat16)
        own_rows = jnp.dot(coarse_inverse, coarse_sum, preferred_element_type=jnp.float32).astype(
            jnp.bfloat16
        )
        coarse_field = lax.all_gather(own_rows, "sy", axis=0, tiled=True)
        picked = jnp.dot(pick_table, coarse_field, preferred_element_type=jnp.float32).astype(
            jnp.bfloat16
        )
        correction = lax.dot_general(
            corners, picked, (((0,), (0,)), ((), ())), preferred_element_type=jnp.float32
        )
        multipliers = (
            multipliers + source - (solved.astype(jnp.float32) - neighbour) - far_term - correction
        )
    interface_field = jnp.dot(
        inverse, multipliers.astype(jnp.bfloat16), preferred_element_type=jnp.float32
    ).astype(jnp.bfloat16)
    return (multipliers.reshape(right_side.shape), interface_field.reshape(right_side.shape))


def solution(mesh):
    return jax.shard_map(
        body,
        mesh=mesh,
        in_specs=(
            P("sx", "sy", "sz", None, None),
            P("sx", "sy", "sz", None, None),
            P("sx", "sy", "sz", None),
            P("sx", "sy", "sz", None, None),
            P("sx", "sy", "sz", None),
            P("sx", "sy", "sz", None, None, None),
            P("sx", "sy", "sz", None, None),
            P("sx", "sy", "sz", None, None),
            P("sx", "sy", "sz", None),
            P("sy", None),
        ),
        out_specs=(P("sx", "sy", "sz", None, None), P("sx", "sy", "sz", None, None)),
        check_vma=False,
    )
```

profile of v0, /device:TPU:1, one launch (start us, length us, event | category | flops | bytes accessed | tf_op | source)
XLA Modules:
  0.0 332.7 jit_solution(17931123030059325352)
XLA Ops:
  11.4 3.7 %fusion.10 = bf16[1536,256]{1,0:T(8,128)(2,1)S(1)} fusion(bf16[1,1,1,1536,1536]{4,3,2,1,0:T(8,128)(2,1)} %param.11, bf16[1,1,1,1536,256]{4,3,2,1,0:T(8,128)(2,1)S(1)} %copy-done.3), kind=kOutput, calls=%fused_computation.16 | convolution fusion | flops 1208352768 | bytes 6291456 | tf_op jit(solution)/shard_map/dot_general | solution.py:75
  18.0 2.5 copy.26
  20.5 2.4 reshape.97
  26.6 13.4 %all-to-all-start = ((bf16[64,3,16,256]{3,2,1,0:T(8,128)(2,1)}), bf16[64,3,16,256]{3,2,1,0:T(8,128)(2,1)}, u32[]{:S(2)}, u32[]{:S(2)}) async-start(bf16[64,3,16,256]{3,2,1,0:T(8,128)(2,1)} %bitcast.102), calls=%async_computation | async-start | bytes 3145728 | tf_op jit(solution)/shard_map/all_to_all | solution.py:89
  41.5 2.3 fusion.29
  43.8 89.8 %all-reduce.2 = bf16[2048,256]{1,0:T(8,128)(2,1)} all-reduce(f32[2048,256]{1,0:T(8,128)} %fusion.29), channel_id=1, replica_groups=mesh['sx'=8,'sy'=4,'sz'=8] {'sx','sy','sz'}, use_global_device_ids=true, to_apply=%region_2.0 | all-reduce | flops 524288 | bytes 3145728 | tf_op jit(solution)/shard_map/psum | solution.py:101
  133.5 3.4 %fusion.24 = bf16[512,256]{0,1:T(8,128)(2,1)} fusion(bf16[512,2048]{1,0:T(8,128)(2,1)} %param.19, bf16[2048,256]{1,0:T(8,128)(2,1)} %all-reduce.2), kind=kOutput, calls=%fused_computation.28 | convolution fusion | flops 537001984 | bytes 3407872 | tf_op jit(solution)/shard_map/dot_general | solution.py:102
  141.3 4.0 %collective-permute-start.2 = (bf16[256,256]{1,0:T(8,128)(2,1)S(1)}, bf16[256,256]{1,0:T(8,128)(2,1)S(1)}, u32[]{:S(2)}, u32[]{:S(2)}) collective-permute-start(bf16[256,256]{1,0:T(8,128)(2,1)S(1)} %get-tuple-element.13), channel_id=1, source_target_pairs={{0,8},{8,16},{16,24},{1,9},{9,17},{17,25},{2,10},{10,18},{18,26},{... | collective-permute-start | bytes 393224 | tf_op jit(solution)/shard_map/ppermute | solution.py:13
  145.3 3.1 collective-permute-start.1
  158.7 3.5 %fusion.9 = f32[1536,256]{1,0:T(8,128)} fusion(bf16[16,256]{1,0:T(8,128)(2,1)S(1)} %reduce_sum.34, f32[1536,256]{1,0:T(8,128)} %broadcast_dynamic-update-slice_fusion.1, bf16[1536,256]{1,0:T(8,128)(2,1)} %copy-done.1, bf16[1,1,1,1536,256]{4,3,2,1,0:T(8,128)(2,1)} %param.10, bf16[1,1,1,16,1536]{4,3,2,1,0:T(8,128)(2,1)S(1)} %copy-done.5), kind=kOutput, calls=%fused_computation.15 | convolution fusion | flops 14942208 | bytes 4775936 | tf_op jit(solution)/shard_map/dot_general | solution.py:93
  162.2 4.0 %fusion.8 = f32[1536,256]{1,0:T(8,128)} fusion(f32[1536,256]{1,0:T(8,128)} %fusion.9, bf16[2048,256]{0,1:T(8,128)(2,1)} %all-gather.3.cloned.1.call-done, s32[8]{0:T(128)S(1)} %bitcast.110, bf16[1,1,1,8,1536]{4,3,2,1,0:T(8,128)(2,1)S(1)} %copy-done.4), kind=kOutput, calls=%fused_computation.13 | convolution fusion | flops 15124480 | bytes 4218912 | tf_op jit(solution)/shard_map/dot_general | solution.py:109
  166.2 4.2 %fusion.13 = bf16[256,1536]{0,1:T(8,128)(2,1)S(1)} fusion(bf16[1,1,1,1536,1536]{4,3,2,1,0:T(8,128)(2,1)} %param.11, f32[1536,256]{1,0:T(8,128)} %fusion.8), kind=kOutput, calls=%fused_computation.17 | convolution fusion | flops 1208745984 | bytes 7077888 | tf_op jit(solution)/shard_map/dot_general | solution.py:75
  173.3 2.5 copy.30
  175.8 2.4 reshape.101
  182.0 9.8 %all-to-all-start.1 = ((bf16[64,3,16,256]{3,2,1,0:T(8,128)(2,1)}), bf16[64,3,16,256]{3,2,1,0:T(8,128)(2,1)}, u32[]{:S(2)}, u32[]{:S(2)}) async-start(bf16[64,3,16,256]{3,2,1,0:T(8,128)(2,1)} %bitcast.103), calls=%async_computation.1 | async-start | bytes 3145728 | tf_op jit(solution)/shard_map/all_to_all | solution.py:89
  193.7 3.5 %collective-permute-start.4 = (bf16[256,256]{1,0:T(8,128)(2,1)}, bf16[256,256]{1,0:T(8,128)(2,1)S(1)}, u32[]{:S(2)}, u32[]{:S(2)}) collective-permute-start(bf16[256,256]{1,0:T(8,128)(2,1)} %get-tuple-element.11), channel_id=1, source_target_pairs={{0,32},{32,64},{64,96},{96,128},{128,160},{160,192},{192,224},{1,3... | collective-permute-start | bytes 393224 | tf_op jit(solution)/shard_map/ppermute | solution.py:13
  198.6 2.3 fusion.28
  200.9 87.7 %all-reduce.3 = bf16[2048,256]{1,0:T(8,128)(2,1)} all-reduce(f32[2048,256]{1,0:T(8,128)} %fusion.28), channel_id=1, replica_groups=mesh['sx'=8,'sy'=4,'sz'=8] {'sx','sy','sz'}, use_global_device_ids=true, to_apply=%region_4.0 | all-reduce | flops 524288 | bytes 3145728 | tf_op jit(solution)/shard_map/psum | solution.py:101
  288.6 3.4 %fusion.25 = bf16[512,256]{0,1:T(8,128)(2,1)} fusion(bf16[512,2048]{1,0:T(8,128)(2,1)} %param.19, bf16[2048,256]{1,0:T(8,128)(2,1)} %all-reduce.3), kind=kOutput, calls=%fused_computation.29 | convolution fusion | flops 537001984 | bytes 3407872 | tf_op jit(solution)/shard_map/dot_general | solution.py:102
  293.3 4.0 %collective-permute-start.6 = (bf16[256,256]{1,0:T(8,128)(2,1)}, bf16[256,256]{1,0:T(8,128)(2,1)S(1)}, u32[]{:S(2)}, u32[]{:S(2)}) collective-permute-start(bf16[256,256]{1,0:T(8,128)(2,1)} %get-tuple-element.9), channel_id=1, source_target_pairs={{0,8},{8,16},{16,24},{1,9},{9,17},{17,25},{2,10},{10,18},{18,26},{... | collective-permute-start | bytes 393224 | tf_op jit(solution)/shard_map/ppermute | solution.py:13
  297.3 3.0 collective-permute-start.5
  310.4 4.0 %fusion.7 = f32[1536,256]{1,0:T(8,128)} fusion(bf16[16,256]{1,0:T(8,128)(2,1)S(1)} %reduce_sum.35, f32[1536,256]{1,0:T(8,128)} %fusion.8, f32[1536,256]{1,0:T(8,128)} %broadcast_dynamic-update-slice_fusion, bf16[1,1,1,1536,256]{4,3,2,1,0:T(8,128)(2,1)} %param.10, bf16[1,1,1,16,1536]{4,3,2,1,0:T(8,128)(2,1)S(1)} %copy-done.5, bf16[256,1536]{0,1:T(8,128)(2,1)} %copy-done.2), kind=kOutput, calls=%fused_computation.11 | convolution fusion | flops 14942208 | bytes 6348800 | tf_op jit(solution)/shard_map/dot_general | solution.py:93
  314.4 4.0 %fusion.6 = f32[1536,256]{1,0:T(8,128)} fusion(f32[1536,256]{1,0:T(8,128)} %fusion.7, bf16[2048,256]{0,1:T(8,128)(2,1)} %all-gather.5.cloned.1.call-done, s32[8]{0:T(128)S(1)} %bitcast.112, bf16[1,1,1,8,1536]{4,3,2,1,0:T(8,128)(2,1)S(1)} %copy-done.4), kind=kOutput, calls=%fused_computation.9 | convolution fusion | flops 15124480 | bytes 4218912 | tf_op jit(solution)/shard_map/dot_general | solution.py:109
  318.4 5.2 %fusion.19 = bf16[1,1,1,1536,256]{3,4,2,1,0:T(8,128)(2,1)} fusion(bf16[1,1,1,1536,1536]{4,3,2,1,0:T(8,128)(2,1)} %param.11, f32[1536,256]{1,0:T(8,128)} %fusion.6), kind=kOutput, calls=%fused_computation.19 | convolution fusion | flops 1208745984 | bytes 7077888 | tf_op jit(solution)/shard_map/dot_general | solution.py:115
  (65 shorter events, 50.2 us)
Async XLA Ops:
  7.2 8.0 %copy-start = (bf16[1,1,1,64,16,1536]{5,4,3,2,1,0:T(8,128)(2,1)S(1)}, bf16[1,1,1,64,16,1536]{5,4,3,2,1,0:T(8,128)(2,1)}, u32[]{:S(2)}) copy-start(bf16[1,1,1,64,16,1536]{5,4,3,2,1,0:T(8,128)(2,1)} %param.15) | copy-start | bytes 9437188
  9.6 1.8 copy-start.3
  15.1 0.9 copy-start.1
  26.6 13.5 %copy-start.4 = (bf16[1,1,1,8,1536]{4,3,2,1,0:T(8,128)(2,1)S(1)}, bf16[1,1,1,8,1536]{4,3,2,1,0:T(8,128)(2,1)}, u32[]{:S(2)}) copy-start(bf16[1,1,1,8,1536]{4,3,2,1,0:T(8,128)(2,1)} %param.17) | copy-start | bytes 73732
  26.6 14.9 %copy-start.6 = (s32[1,1,1,8]{3,2,1,0:T(1,128)S(1)}, s32[1,1,1,8]{3,2,1,0:T(1,128)}, u32[]{:S(2)}) copy-start(s32[1,1,1,8]{3,2,1,0:T(1,128)} %param.18) | copy-start | bytes 100
  26.6 130.4 %all-to-all-start = ((bf16[64,3,16,256]{3,2,1,0:T(8,128)(2,1)}), bf16[64,3,16,256]{3,2,1,0:T(8,128)(2,1)}, u32[]{:S(2)}, u32[]{:S(2)}) async-start(bf16[64,3,16,256]{3,2,1,0:T(8,128)(2,1)} %bitcast.102), calls=%async_computation | async-start | bytes 3145728 | tf_op jit(solution)/shard_map/all_to_all | solution.py:89
  40.1 122.1 %all-gather.3.cloned.1.call-start = ((), (), s32[]{:S(2)}) async-start(), calls=%async_computation.2 | async-start | bytes 1310720 | tf_op jit(solution)/shard_map/all_gather | solution.py:105
  133.5 15.0 %copy-start.7 = (s32[1,1,1,4]{3,2,1,0:T(1,128)S(1)}, s32[1,1,1,4]{3,2,1,0:T(1,128)}, u32[]{:S(2)}) copy-start(s32[1,1,1,4]{3,2,1,0:T(1,128)} %param.12) | copy-start | bytes 52
  138.1 11.0 %collective-permute-start = (bf16[256,256]{1,0:T(8,128)(2,1)S(1)}, bf16[256,256]{1,0:T(8,128)(2,1)S(1)}, u32[]{:S(2)}, u32[]{:S(2)}) collective-permute-start(bf16[256,256]{1,0:T(8,128)(2,1)S(1)} %get-tuple-element.15), channel_id=1, source_target_pairs={{0,32},{32,64},{64,96},{96,128},{128,160},{160,192},{192,224},{1,3... | collective-permute-start | bytes 393224 | tf_op jit(solution)/shard_map/ppermute | solution.py:13
  140.0 14.7 %collective-permute-start.3 = (bf16[256,256]{1,0:T(8,128)(2,1)S(1)}, bf16[256,256]{1,0:T(8,128)(2,1)S(1)}, u32[]{:S(2)}, u32[]{:S(2)}) collective-permute-start(bf16[256,256]{1,0:T(8,128)(2,1)S(1)} %get-tuple-element.12), channel_id=1, source_target_pairs={{8,0},{16,8},{24,16},{9,1},{17,9},{25,17},{10,2},{18,10},{26,18},{... | collective-permute-start | bytes 393224 | tf_op jit(solution)/shard_map/ppermute | solution.py:13
  141.3 12.0 %collective-permute-start.2 = (bf16[256,256]{1,0:T(8,128)(2,1)S(1)}, bf16[256,256]{1,0:T(8,128)(2,1)S(1)}, u32[]{:S(2)}, u32[]{:S(2)}) collective-permute-start(bf16[256,256]{1,0:T(8,128)(2,1)S(1)} %get-tuple-element.13), channel_id=1, source_target_pairs={{0,8},{8,16},{16,24},{1,9},{9,17},{17,25},{2,10},{10,18},{18,26},{... | collective-permute-start | bytes 393224 | tf_op jit(solution)/shard_map/ppermute | solution.py:13
  145.3 6.7 %collective-permute-start.1 = (bf16[256,256]{1,0:T(8,128)(2,1)S(1)}, bf16[256,256]{1,0:T(8,128)(2,1)S(1)}, u32[]{:S(2)}, u32[]{:S(2)}) collective-permute-start(bf16[256,256]{1,0:T(8,128)(2,1)S(1)} %get-tuple-element.14), channel_id=1, source_target_pairs={{32,0},{64,32},{96,64},{128,96},{160,128},{192,160},{224,192},{33,... | collective-permute-start | bytes 393224 | tf_op jit(solution)/shard_map/ppermute | solution.py:13
  152.0 6.7 %copy-start.5 = (bf16[1,1,1,16,1536]{4,3,2,1,0:T(8,128)(2,1)S(1)}, bf16[1,1,1,16,1536]{4,3,2,1,0:T(8,128)(2,1)}, u32[]{:S(2)}) copy-start(bf16[1,1,1,16,1536]{4,3,2,1,0:T(8,128)(2,1)} %param.16) | copy-start | bytes 147460
  170.4 0.9 copy-start.2
  182.0 126.8 %all-to-all-start.1 = ((bf16[64,3,16,256]{3,2,1,0:T(8,128)(2,1)}), bf16[64,3,16,256]{3,2,1,0:T(8,128)(2,1)}, u32[]{:S(2)}, u32[]{:S(2)}) async-start(bf16[64,3,16,256]{3,2,1,0:T(8,128)(2,1)} %bitcast.103), calls=%async_computation.1 | async-start | bytes 3145728 | tf_op jit(solution)/shard_map/all_to_all | solution.py:89
  191.8 122.6 %all-gather.5.cloned.1.call-start = ((), (), s32[]{:S(2)}) async-start(), calls=%async_computation.3 | async-start | bytes 1310720 | tf_op jit(solution)/shard_map/all_gather | solution.py:105
  193.7 106.6 %collective-permute-start.4 = (bf16[256,256]{1,0:T(8,128)(2,1)}, bf16[256,256]{1,0:T(8,128)(2,1)S(1)}, u32[]{:S(2)}, u32[]{:S(2)}) collective-permute-start(bf16[256,256]{1,0:T(8,128)(2,1)} %get-tuple-element.11), channel_id=1, source_target_pairs={{0,32},{32,64},{64,96},{96,128},{128,160},{160,192},{192,224},{1,3... | collective-permute-start | bytes 393224 | tf_op jit(solution)/shard_map/ppermute | solution.py:13
  292.0 14.5 %collective-permute-start.7 = (bf16[256,256]{1,0:T(8,128)(2,1)S(1)}, bf16[256,256]{1,0:T(8,128)(2,1)S(1)}, u32[]{:S(2)}, u32[]{:S(2)}) collective-permute-start(bf16[256,256]{1,0:T(8,128)(2,1)S(1)} %get-tuple-element.8), channel_id=1, source_target_pairs={{8,0},{16,8},{24,16},{9,1},{17,9},{25,17},{10,2},{18,10},{26,18},{... | collective-permute-start | bytes 393224 | tf_op jit(solution)/shard_map/ppermute | solution.py:13
  293.3 11.8 %collective-permute-start.6 = (bf16[256,256]{1,0:T(8,128)(2,1)}, bf16[256,256]{1,0:T(8,128)(2,1)S(1)}, u32[]{:S(2)}, u32[]{:S(2)}) collective-permute-start(bf16[256,256]{1,0:T(8,128)(2,1)} %get-tuple-element.9), channel_id=1, source_target_pairs={{0,8},{8,16},{16,24},{1,9},{9,17},{17,25},{2,10},{10,18},{18,26},{... | collective-permute-start | bytes 393224 | tf_op jit(solution)/shard_map/ppermute | solution.py:13
  297.3 6.5 %collective-permute-start.5 = (bf16[256,256]{1,0:T(8,128)(2,1)}, bf16[256,256]{1,0:T(8,128)(2,1)S(1)}, u32[]{:S(2)}, u32[]{:S(2)}) collective-permute-start(bf16[256,256]{1,0:T(8,128)(2,1)} %get-tuple-element.10), channel_id=1, source_target_pairs={{32,0},{64,32},{96,64},{128,96},{160,128},{192,160},{224,192},{33,... | collective-permute-start | bytes 393224 | tf_op jit(solution)/shard_map/ppermute | solution.py:13
Sparse Core Ops, SparseCore 0:
  137.1 21.9 all-gather.2
  292.1 21.2 all-gather.4
where the time goes:
time: 334 us; the launch traced here: 333 us
  blocking collectives  177 us (53%)
  matrix products  50.9 us (15%)
  starting transfers between devices  45.5 us (14%)
  local copies, waits for them, and re-layouts  24.3 us (7%)
  other arithmetic  16.6 us (5%)
  between operations  14.3 us (4%)
  waiting for transfers between devices  3.7 us (1%)
    psum x2, blocking collectives, body(): coarse_sum = lax.psum(partial_sum, ('sx', 'sy', 'sz')).astype(jnp.bfloat16)  177 us
    all_to_all x2, starting transfers between devices, body(): lax.all_to_all(outgoing, ('sx', 'sz'), split_axis=0, concat_axis=0, tiled...  23.3 us
    ppermute x8, starting transfers between devices, shifted(): return lax.ppermute(block, axis, route)  22.2 us
    dot_general x3, matrix products, body(): jnp.dot(inverse, multipliers.astype(jnp.bfloat16), preferred_element_type...  13.1 us
    unnamed x8, other arithmetic  10.9 us
    unnamed x20, local copies, waits for them, and re-layouts  8.84 us
    dot_general x2, matrix products, body(): lax.dot_general(corners, picked, (((0,), (0,)), ((), ())), preferred_elem...  7.96 us
    dot_general x2, matrix products, body(): lax.dot_general(patch, arrived.astype(jnp.bfloat16), (((0,), (0,)), ((),...  7.48 us
  transfers between devices with their start and end apart: 12, of which 2 were waited for; matrix products, arithmetic and copies ran while one was open for 12% of the time, Pallas kernels for 0%

commit v1 on v0

v1 whole, which is shorter than its diff:
```python
import jax
import jax.numpy as jnp
from jax import lax
from jax.sharding import Mesh
from jax.sharding import PartitionSpec as P

ITERS = 2
RADIX = 64
GRID = ("y", "core")
BULK = ("y", "z")
LINE = ("core", "x")


def shifted(block, axis, distance):
    devices = range(lax.axis_size(axis))
    route = [(i - distance, i) for i in devices if i - distance in devices]
    return lax.ppermute(block, axis, route)


def swapped(block):
    return lax.ppermute(block, "core", [(0, 1), (1, 0)])


def exchanged(block, axis):
    return lax.all_to_all(block, axis, split_axis=0, concat_axis=0, tiled=True)


def product(left, right, dims=((1,), (0,))):
    return lax.dot_general(left, right, (dims, ((), ())), preferred_element_type=jnp.float32)


def written_ids(ids, columns):
    half = (ids.shape[0], columns // 2)
    high = jnp.broadcast_to((ids // RADIX)[:, None], half)
    low = jnp.broadcast_to((ids % RADIX)[:, None], half)
    return jnp.concatenate([high, low], axis=1).astype(jnp.bfloat16)


def read_ids(rows):
    middle = rows.shape[1] // 2
    pair = rows.astype(jnp.int32)
    return pair[:, :1] * RADIX + pair[:, middle : middle + 1]


def body(
    right_side,
    interface_inverse,
    face_link,
    far_target,
    far_rank,
    far_basis,
    patch_basis,
    corner_basis,
    corner_row,
    coarse_inverse,
):
    order = interface_inverse.shape[-1]
    columns = right_side.shape[-1]
    face_rows = order // 6
    inverse = interface_inverse.reshape(order, order)
    source = right_side.reshape(order, columns)
    links = face_link.reshape(4).astype(jnp.float32)
    rank_limit = far_basis.shape[-2]
    bases = far_basis.reshape(-1, order)
    patch = patch_basis.reshape(rank_limit, order)
    corners = corner_basis.reshape(-1, order)
    corner_count = corners.shape[0]
    ids = corner_row.reshape(-1)
    own_coarse, coarse_order = coarse_inverse.shape
    depth = lax.axis_size("z")
    bulk = lax.axis_size("y") * depth
    line = lax.axis_size("x")
    core = lax.axis_index("core")

    targets = far_target.reshape(-1, 1)
    ranks = far_rank.reshape(-1, 1)
    sides = jnp.bitwise_xor((targets // depth) % 2, core)
    places = sides * bulk + (targets // (2 * depth)) * depth + targets % depth
    row = jnp.arange(rank_limit, dtype=jnp.int32)[None, :]
    key = jnp.where(row < ranks, places * rank_limit + row, -1).reshape(1, -1)
    spots = 2 * bulk * rank_limit
    route = (jnp.arange(spots, dtype=jnp.int32)[:, None] == key).astype(jnp.bfloat16)

    id_rows = written_ids(ids, columns)
    line_ids = read_ids(
        exchanged(jnp.broadcast_to(id_rows[None], (line,) + id_rows.shape), "x").reshape(-1, columns)
    )
    local = line_ids - lax.axis_index("x") * own_coarse
    hot = (local == jnp.arange(own_coarse, dtype=jnp.int32)[None, :]).astype(jnp.bfloat16)
    held = product(hot, coarse_inverse).astype(jnp.bfloat16)
    spread = exchanged(jnp.broadcast_to(held[None], (line,) + held.shape), "x")
    own_rows = jnp.sum(spread.astype(jnp.float32), axis=0).astype(jnp.bfloat16)
    other_rows = swapped(own_rows)
    coarse_rows = jnp.where(
        core == 0,
        jnp.concatenate([own_rows, other_rows], axis=0),
        jnp.concatenate([other_rows, own_rows], axis=0),
    )

    multipliers = source.astype(jnp.float32)
    rounded = source
    coupling = None
    for sweep in range(ITERS):
        solved = product(inverse, rounded).astype(jnp.bfloat16)
        coefficient = product(bases, solved).astype(jnp.bfloat16)
        half = spots // 2
        outgoing = product(route[half:], coefficient).astype(jnp.bfloat16)
        incoming = swapped(outgoing)
        kept = product(route[:half], coefficient)
        far_rows = (kept + incoming.astype(jnp.float32)).astype(jnp.bfloat16)
        terms = product(corners, solved).astype(jnp.bfloat16)
        extra = terms if coupling is not None else jnp.concatenate([terms, id_rows], axis=0)
        payload = jnp.concatenate(
            [
                far_rows.reshape(bulk, rank_limit, columns),
                jnp.broadcast_to(extra[None], (bulk,) + extra.shape),
            ],
            axis=1,
        )
        landed = exchanged(payload, BULK)
        arrived = jnp.sum(landed[:, :rank_limit].astype(jnp.float32), axis=0).astype(jnp.bfloat16)
        last = rank_limit + corner_count
        all_terms = landed[:, rank_limit:last].reshape(-1, columns)
        if coupling is None:
            all_ids = read_ids(landed[:, last:].reshape(-1, columns))
            placed = (all_ids == jnp.arange(coarse_order, dtype=jnp.int32)[None, :]).astype(
                jnp.bfloat16
            )
            coupling = product(coarse_rows, placed, ((1,), (1,))).astype(jnp.bfloat16)
        partial = product(coupling, all_terms).astype(jnp.bfloat16)
        shares = exchanged(partial.reshape(-1, corner_count, columns), LINE)
        picked = jnp.sum(shares.astype(jnp.float32), axis=0).astype(jnp.bfloat16)

        pieces = []
        for offset, sent_face, axis in ((1, 1, GRID), (-1, 0, GRID), (1, 3, "x"), (-1, 2, "x")):
            sent = solved[sent_face * face_rows : (sent_face + 1) * face_rows]
            pieces.append(shifted(sent, axis, offset).astype(jnp.float32) * links[len(pieces)])
        pieces.append(jnp.zeros((order - 4 * face_rows, columns), jnp.float32))
        neighbour = jnp.concatenate(pieces, axis=0)
        far_term = product(patch, arrived, ((0,), (0,)))
        correction = product(corners, picked, ((0,), (0,)))
        multipliers = (
            multipliers
            + source.astype(jnp.float32)
            - (solved.astype(jnp.float32) - neighbour)
            - far_term
            - correction
        )
        rounded = multipliers.astype(jnp.bfloat16)
    field = product(inverse, rounded).astype(jnp.bfloat16)
    return multipliers.reshape(right_side.shape), field.reshape(right_side.shape)


def solution(mesh):
    sizes = mesh.shape
    fine = Mesh(
        mesh.devices.reshape(sizes["sx"] // 2, 2, sizes["sy"], sizes["sz"]), ("y", "core", "x", "z")
    )
    sub = P(GRID, "x", "z")
    return jax.shard_map(
        body,
        mesh=fine,
        in_specs=(sub,) * 9 + (P("x", None),),
        out_specs=(sub, sub),
        check_vma=False,
    )
```

time: 334 us -> 156 us (0.47)
  blocking collectives: 177 us -> 0 us
  starting transfers between devices: 45.5 us -> 66 us
  matrix products: 50.9 us -> 37 us
  between operations: 14.3 us -> 1.05 us
  local copies, waits for them, and re-layouts: 24.3 us -> 12.2 us
  waiting for transfers between devices: 3.7 us -> 15.1 us
  other arithmetic: 16.6 us -> 22.8 us
    psum x2 -> x0, blocking collectives: 177 us -> none  [body(): coarse_sum = lax.psum(partial_sum, ('sx', 'sy', 'sz')).astype(jnp.bfloat16)]
    all_to_all x2 -> x6, starting transfers between devices: 23.3 us -> 40.5 us  [exchanged(): return lax.all_to_all(block, axis, split_axis=0, concat_axis=0, tiled=True)]
    all_to_all x2 -> x6, waiting for transfers between devices: 0.01 us -> 15.1 us  [exchanged(): return lax.all_to_all(block, axis, split_axis=0, concat_axis=0, tiled=True)]
    dot_general x17 -> x19, matrix products: 50.9 us -> 37 us  [product(): lax.dot_general(left, right, (dims, ((), ())), preferred_element_type=jnp...]
    dot_general x2 -> x0, local copies, waits for them, and re-layouts: 5.09 us -> none  [body(): jnp.dot(bases, solved, preferred_element_type=jnp.float32)]
    reshape x2 -> x0, local copies, waits for them, and re-layouts: 4.8 us -> none  [body(): jnp.dot(bases, solved, preferred_element_type=jnp.float32)]
    unnamed x8, other arithmetic: 10.9 us -> 15.3 us
    ppermute x8, waiting for transfers between devices: 3.66 us -> 0.02 us  [shifted(): return lax.ppermute(block, axis, route)]
  transfers between devices with their start and end apart: 12 -> 17, of which waited for: 2 -> 5; matrix products, arithmetic and copies ran while one was open for 12% -> 30% of each run, Pallas kernels for 0% -> 0%
where the time goes in v1:
time: 156 us; the launch traced here: 154 us
  starting transfers between devices  66 us (42%)
  matrix products  37 us (24%)
  other arithmetic  22.8 us (15%)
  waiting for transfers between devices  15.1 us (10%)
  local copies, waits for them, and re-layouts  12.2 us (8%)
    all_to_all x6, starting transfers between devices, exchanged(): return lax.all_to_all(block, axis, split_axis=0, concat_axis=0, tiled=True)  40.5 us
    dot_general x19, matrix products, product(): lax.dot_general(left, right, (dims, ((), ())), preferred_element_type=jnp...  37 us
    ppermute x8, starting transfers between devices, shifted(): return lax.ppermute(block, axis, route)  22.6 us
    unnamed x8, other arithmetic  15.3 us
    all_to_all x6, waiting for transfers between devices, exchanged(): return lax.all_to_all(block, axis, split_axis=0, concat_axis=0, tiled=True)  15.1 us
    unnamed x33, local copies, waits for them, and re-layouts  6.57 us
  transfers between devices with their start and end apart: 17, of which 5 were waited for; matrix products, arithmetic and copies ran while one was open for 30% of the time, Pallas kernels for 0%

profile of v1, /device:TPU:1, one launch (start us, length us, event | category | flops | bytes accessed | tf_op | source)
XLA Modules:
  0.0 154.1 jit_solution(9309899462353280846)
XLA Ops:
  2.2 4.8 %all-to-all-start.1 = ((bf16[4,8,256]{2,1,0:T(8,128)(2,1)}), bf16[4,8,256]{2,1,0:T(8,128)(2,1)S(1)}, u32[]{:S(2)}, u32[]{:S(2)}) async-start(bf16[4,8,256]{2,1,0:T(8,128)(2,1)} %broadcast_in_dim.20), calls=%async_computation.1 | async-start | bytes 32768 | tf_op jit(solution)/shard_map/all_to_all | solution.py:25
  7.1 4.0 %fusion.10 = bf16[1536,256]{1,0:T(8,128)(2,1)S(1)} fusion(bf16[1,1,1,1536,1536]{4,3,2,1,0:T(8,128)(2,1)} %param.11, bf16[1,1,1,1536,256]{4,3,2,1,0:T(8,128)(2,1)} %param.10), kind=kOutput, calls=%fused_computation.15 | convolution fusion | flops 1208352768 | bytes 6291456 | tf_op jit(solution)/shard_map/dot_general | solution.py:29
  14.0 4.0 %collective-permute-start.2 = (bf16[256,256]{1,0:T(8,128)(2,1)}, bf16[256,256]{1,0:T(8,128)(2,1)S(1)}, u32[]{:S(2)}, u32[]{:S(2)}) collective-permute-start(bf16[256,256]{1,0:T(8,128)(2,1)} %get-tuple-element.15), channel_id=1, source_target_pairs={{0,8},{8,16},{16,24},{1,9},{9,17},{17,25},{2,10},{10,18},{18,26},{... | collective-permute-start | bytes 393224 | tf_op jit(solution)/shard_map/ppermute | solution.py:17
  18.0 4.1 %collective-permute-start.1 = (bf16[256,256]{1,0:T(8,128)(2,1)}, bf16[256,256]{1,0:T(8,128)(2,1)}, u32[]{:S(2)}, u32[]{:S(2)}) collective-permute-start(bf16[256,256]{1,0:T(8,128)(2,1)} %get-tuple-element.16), channel_id=1, source_target_pairs={{32,0},{64,32},{96,64},{128,96},{160,128},{192,160},{224,192},{33,... | collective-permute-start | bytes 393224 | tf_op jit(solution)/shard_map/ppermute | solution.py:17
  22.1 2.4 %collective-permute-start = (bf16[256,256]{1,0:T(8,128)(2,1)}, bf16[256,256]{1,0:T(8,128)(2,1)}, u32[]{:S(2)}, u32[]{:S(2)}) collective-permute-start(bf16[256,256]{1,0:T(8,128)(2,1)} %get-tuple-element.17), channel_id=1, source_target_pairs={{0,32},{32,64},{64,96},{96,128},{128,160},{160,192},{192,224},{1,3... | collective-permute-start | bytes 393224 | tf_op jit(solution)/shard_map/ppermute | solution.py:17
  33.6 4.5 %all-to-all-start.2 = ((bf16[4,32,2048]{2,1,0:T(8,128)(2,1)}), bf16[4,32,2048]{2,1,0:T(8,128)(2,1)}, u32[]{:S(2)}, u32[]{:S(2)}) async-start(bf16[4,32,2048]{2,1,0:T(8,128)(2,1)} %broadcast_in_dim.21), calls=%async_computation.2 | async-start | bytes 1048576 | tf_op jit(solution)/shard_map/all_to_all | solution.py:25
  40.8 6.3 %all-to-all-done.2 = bf16[4,32,2048]{2,1,0:T(8,128)(2,1)} async-done(((bf16[4,32,2048]{2,1,0:T(8,128)(2,1)}), bf16[4,32,2048]{2,1,0:T(8,128)(2,1)}, u32[]{:S(2)}, u32[]{:S(2)}) %all-to-all-start.2) | async-done | bytes 524320 | tf_op jit(solution)/shard_map/all_to_all | solution.py:25
  47.1 11.0 %all-to-all-start = ((bf16[32,32,256]{2,1,0:T(8,128)(2,1)}), bf16[32,32,256]{2,1,0:T(8,128)(2,1)}, u32[]{:S(2)}, u32[]{:S(2)}) async-start(bf16[32,32,256]{2,1,0:T(8,128)(2,1)} %pad_maximum_fusion), calls=%async_computation | async-start | bytes 1048576 | tf_op jit(solution)/shard_map/all_to_all | solution.py:25
  58.2 2.3 %multiply_dynamic-update-slice_fusion.7 = f32[1536,256]{1,0:T(8,128)} fusion(bf16[256,256]{1,0:T(8,128)(2,1)} %collective-permute-done, f32[]{:T(128)} %bitcast.2), kind=kLoop, calls=%fused_computation.72 | loop fusion | flops 131071 | bytes 393220
  60.5 2.2 %multiply_dynamic-update-slice_fusion.6 = f32[1536,256]{1,0:T(8,128)} fusion(f32[1536,256]{1,0:T(8,128)} %multiply_dynamic-update-slice_fusion.7, bf16[256,256]{1,0:T(8,128)(2,1)} %collective-permute-done.1, f32[]{:T(128)} %bitcast.3), kind=kLoop, calls=%fused_computation.71 | loop fusion | flops 131072 | bytes 393728
  69.0 3.1 %all-to-all-done = bf16[32,32,256]{2,1,0:T(8,128)(2,1)} async-done(((bf16[32,32,256]{2,1,0:T(8,128)(2,1)}), bf16[32,32,256]{2,1,0:T(8,128)(2,1)}, u32[]{:S(2)}, u32[]{:S(2)}) %all-to-all-start) | async-done | bytes 524320 | tf_op jit(solution)/shard_map/all_to_all | solution.py:25
  76.1 7.4 %all-to-all-start.3 = ((bf16[8,8,256]{2,1,0:T(8,128)(2,1)}), bf16[8,8,256]{2,1,0:T(8,128)(2,1)S(1)}, u32[]{:S(2)}, u32[]{:S(2)}) async-start(bf16[8,8,256]{2,1,0:T(8,128)(2,1)} %fusion.40), calls=%async_computation.3 | async-start | bytes 65536 | tf_op jit(solution)/shard_map/all_to_all | solution.py:25
  84.4 3.5 %fusion.9 = f32[1536,256]{1,0:T(8,128)} fusion(bf16[16,256]{1,0:T(8,128)(2,1)S(1)} %slice_reduce_fusion.1, f32[1536,256]{1,0:T(8,128)} %broadcast_dynamic-update-slice_fusion.1, bf16[1536,256]{1,0:T(8,128)(2,1)} %copy-done.2, bf16[1,1,1,1536,256]{4,3,2,1,0:T(8,128)(2,1)} %param.10, bf16[1,1,1,16,1536]{4,3,2,1,0:T(8,128)(2,1)S(1)} %copy-done.10), kind=kOutput, calls=%fused_computation.14 | convolution fusion | flops 14942208 | bytes 4775936 | tf_op jit(solution)/shard_map/dot_general | solution.py:29
  91.3 3.7 %fusion.13 = bf16[256,1536]{0,1:T(8,128)(2,1)S(1)} fusion(bf16[1,1,1,1536,1536]{4,3,2,1,0:T(8,128)(2,1)} %param.11, f32[1536,256]{1,0:T(8,128)S(1)} %fusion.8), kind=kOutput, calls=%fused_computation.16 | convolution fusion | flops 1208745984 | bytes 7077888 | tf_op jit(solution)/shard_map/dot_general | solution.py:29
  101.9 4.7 %collective-permute-start.8 = (bf16[256,256]{1,0:T(8,128)(2,1)}, bf16[256,256]{1,0:T(8,128)(2,1)}, u32[]{:S(2)}, u32[]{:S(2)}) collective-permute-start(bf16[256,256]{1,0:T(8,128)(2,1)} %get-tuple-element.11), channel_id=1, source_target_pairs={{0,8},{8,16},{16,24},{1,9},{9,17},{17,25},{2,10},{10,18},{18,26},{... | collective-permute-start | bytes 393224 | tf_op jit(solution)/shard_map/ppermute | solution.py:17
  106.6 3.0 %collective-permute-start.7 = (bf16[256,256]{1,0:T(8,128)(2,1)}, bf16[256,256]{1,0:T(8,128)(2,1)}, u32[]{:S(2)}, u32[]{:S(2)}) collective-permute-start(bf16[256,256]{1,0:T(8,128)(2,1)} %get-tuple-element.12), channel_id=1, source_target_pairs={{32,0},{64,32},{96,64},{128,96},{160,128},{192,160},{224,192},{33,... | collective-permute-start | bytes 393224 | tf_op jit(solution)/shard_map/ppermute | solution.py:17
  112.3 5.4 %all-to-all-start.4 = ((bf16[32,24,256]{2,1,0:T(8,128)(2,1)}), bf16[32,24,256]{2,1,0:T(8,128)(2,1)S(1)}, u32[]{:S(2)}, u32[]{:S(2)}) async-start(bf16[32,24,256]{2,1,0:T(8,128)(2,1)} %pad_maximum_fusion.1), calls=%async_computation.4 | async-start | bytes 786432 | tf_op jit(solution)/shard_map/all_to_all | solution.py:25
  117.7 2.2 %multiply_dynamic-update-slice_fusion.2 = f32[1536,256]{1,0:T(8,128)} fusion(f32[1536,256]{1,0:T(8,128)} %multiply_dynamic-update-slice_fusion.3, bf16[256,256]{1,0:T(8,128)(2,1)} %collective-permute-done.7, f32[]{:T(128)} %bitcast.3), kind=kLoop, calls=%fused_computation.65 | loop fusion | flops 131072 | bytes 393728
  120.0 2.2 %multiply_dynamic-update-slice_fusion.1 = f32[1536,256]{1,0:T(8,128)} fusion(f32[1536,256]{1,0:T(8,128)} %multiply_dynamic-update-slice_fusion.2, bf16[256,256]{1,0:T(8,128)(2,1)} %collective-permute-done.8, f32[]{:T(128)} %bitcast.4), kind=kLoop, calls=%fused_computation.64 | loop fusion | flops 131072 | bytes 393728
  125.3 4.3 %all-to-all-done.4 = bf16[32,24,256]{2,1,0:T(8,128)(2,1)S(1)} async-done(((bf16[32,24,256]{2,1,0:T(8,128)(2,1)}), bf16[32,24,256]{2,1,0:T(8,128)(2,1)S(1)}, u32[]{:S(2)}, u32[]{:S(2)}) %all-to-all-start.4) | async-done | bytes 393248 | tf_op jit(solution)/shard_map/all_to_all | solution.py:25
  131.0 7.3 %all-to-all-start.5 = ((bf16[8,8,256]{2,1,0:T(8,128)(2,1)}), bf16[8,8,256]{2,1,0:T(8,128)(2,1)}, u32[]{:S(2)}, u32[]{:S(2)}) async-start(bf16[8,8,256]{2,1,0:T(8,128)(2,1)} %fusion.41), calls=%async_computation.5 | async-start | bytes 65536 | tf_op jit(solution)/shard_map/all_to_all | solution.py:25
  138.4 4.0 %fusion.7 = f32[1536,256]{1,0:T(8,128)} fusion(bf16[16,256]{1,0:T(8,128)(2,1)S(1)} %slice_reduce_fusion, f32[1536,256]{1,0:T(8,128)} %copy-done.1, f32[1536,256]{1,0:T(8,128)} %broadcast_dynamic-update-slice_fusion, bf16[1,1,1,1536,256]{4,3,2,1,0:T(8,128)(2,1)} %param.10, bf16[1,1,1,16,1536]{4,3,2,1,0:T(8,128)(2,1)} %param.16, bf16[256,1536]{0,1:T(8,128)(2,1)} %copy-done.4), kind=kOutput, calls=%fused_computation.10 | convolution fusion | flops 14942208 | bytes 6348800 | tf_op jit(solution)/shard_map/dot_general | solution.py:29
  147.2 4.7 %fusion.19 = bf16[1,1,1,1536,256]{3,4,2,1,0:T(8,128)(2,1)} fusion(bf16[1,1,1,1536,1536]{4,3,2,1,0:T(8,128)(2,1)} %param.11, f32[1536,256]{1,0:T(8,128)S(1)} %fusion.6), kind=kOutput, calls=%fused_computation.18 | convolution fusion | flops 1208745984 | bytes 7077888 | tf_op jit(solution)/shard_map/dot_general | solution.py:29
  151.8 2.3 %copy.37 = bf16[1,1,1,1536,256]{4,3,2,1,0:T(8,128)(2,1)} copy(bf16[1,1,1,1536,256]{3,4,2,1,0:T(8,128)(2,1)} %fusion.19) | data formatting | bytes 1572864
  (100 shorter events, 49.6 us)
Async XLA Ops:
  0.6 24.1 %copy-start = (bf16[1,1,1,64,16,1536]{5,4,3,2,1,0:T(8,128)(2,1)S(1)}, bf16[1,1,1,64,16,1536]{5,4,3,2,1,0:T(8,128)(2,1)}, u32[]{:S(2)}) copy-start(bf16[1,1,1,64,16,1536]{5,4,3,2,1,0:T(8,128)(2,1)} %param.15) | copy-start | bytes 9437188
  2.2 28.3 %all-to-all-start.1 = ((bf16[4,8,256]{2,1,0:T(8,128)(2,1)}), bf16[4,8,256]{2,1,0:T(8,128)(2,1)S(1)}, u32[]{:S(2)}, u32[]{:S(2)}) async-start(bf16[4,8,256]{2,1,0:T(8,128)(2,1)} %broadcast_in_dim.20), calls=%async_computation.1 | async-start | bytes 32768 | tf_op jit(solution)/shard_map/all_to_all | solution.py:25
  7.0 17.5 %copy-start.13 = (s32[1,1,1,64,1]{3,4,2,1,0:T(1,128)S(1)}, s32[1,1,1,64,1]{3,4,2,1,0:T(1,128)}, u32[]{:S(2)}) copy-start(s32[1,1,1,64,1]{3,4,2,1,0:T(1,128)} %param.13) | copy-start | bytes 772
  7.1 17.5 %copy-start.12 = (s32[1,1,1,64]{3,2,1,0:T(1,128)S(1)}, s32[1,1,1,64]{3,2,1,0:T(1,128)}, u32[]{:S(2)}) copy-start(s32[1,1,1,64]{3,2,1,0:T(1,128)} %param.14) | copy-start | bytes 772
  12.7 51.4 %collective-permute-start.3 = (bf16[256,256]{1,0:T(8,128)(2,1)}, bf16[256,256]{1,0:T(8,128)(2,1)S(1)}, u32[]{:S(2)}, u32[]{:S(2)}) collective-permute-start(bf16[256,256]{1,0:T(8,128)(2,1)} %get-tuple-element.14), channel_id=1, source_target_pairs={{8,0},{16,8},{24,16},{9,1},{17,9},{25,17},{10,2},{18,10},{26,18},{... | collective-permute-start | bytes 393224 | tf_op jit(solution)/shard_map/ppermute | solution.py:17
  14.0 48.7 %collective-permute-start.2 = (bf16[256,256]{1,0:T(8,128)(2,1)}, bf16[256,256]{1,0:T(8,128)(2,1)S(1)}, u32[]{:S(2)}, u32[]{:S(2)}) collective-permute-start(bf16[256,256]{1,0:T(8,128)(2,1)} %get-tuple-element.15), channel_id=1, source_target_pairs={{0,8},{8,16},{16,24},{1,9},{9,17},{17,25},{2,10},{10,18},{18,26},{... | collective-permute-start | bytes 393224 | tf_op jit(solution)/shard_map/ppermute | solution.py:17
  18.0 42.5 %collective-permute-start.1 = (bf16[256,256]{1,0:T(8,128)(2,1)}, bf16[256,256]{1,0:T(8,128)(2,1)}, u32[]{:S(2)}, u32[]{:S(2)}) collective-permute-start(bf16[256,256]{1,0:T(8,128)(2,1)} %get-tuple-element.16), channel_id=1, source_target_pairs={{32,0},{64,32},{96,64},{128,96},{160,128},{192,160},{224,192},{33,... | collective-permute-start | bytes 393224 | tf_op jit(solution)/shard_map/ppermute | solution.py:17
  22.1 36.1 %collective-permute-start = (bf16[256,256]{1,0:T(8,128)(2,1)}, bf16[256,256]{1,0:T(8,128)(2,1)}, u32[]{:S(2)}, u32[]{:S(2)}) collective-permute-start(bf16[256,256]{1,0:T(8,128)(2,1)} %get-tuple-element.17), channel_id=1, source_target_pairs={{0,32},{32,64},{64,96},{96,128},{128,160},{160,192},{192,224},{1,3... | collective-permute-start | bytes 393224 | tf_op jit(solution)/shard_map/ppermute | solution.py:17
  26.9 2.1 %copy-start.15 = (bf16[256,1024]{1,0:T(8,128)(2,1)}, bf16[256,1024]{1,0:T(8,128)(2,1)S(1)}, u32[]{:S(2)}) copy-start(bf16[256,1024]{1,0:T(8,128)(2,1)S(1)} %convolution_convert_fusion.2) | copy-start | bytes 1572868
  29.0 9.0 %collective-permute-start.4 = (bf16[512,256]{1,0:T(8,128)(2,1)}, bf16[512,256]{1,0:T(8,128)(2,1)}, u32[]{:S(2)}, u32[]{:S(2)}) collective-permute-start(bf16[512,256]{1,0:T(8,128)(2,1)} %fusion.33), channel_id=1, source_target_pairs={{0,32},{32,0},{1,33},{33,1},{2,34},{34,2},{3,35},{35,3},{4,36},{36... | collective-permute-start | bytes 786440 | tf_op jit(solution)/shard_map/ppermute | solution.py:21
  33.6 13.5 %all-to-all-start.2 = ((bf16[4,32,2048]{2,1,0:T(8,128)(2,1)}), bf16[4,32,2048]{2,1,0:T(8,128)(2,1)}, u32[]{:S(2)}, u32[]{:S(2)}) async-start(bf16[4,32,2048]{2,1,0:T(8,128)(2,1)} %broadcast_in_dim.21), calls=%async_computation.2 | async-start | bytes 1048576 | tf_op jit(solution)/shard_map/all_to_all | solution.py:25
  47.1 25.0 %all-to-all-start = ((bf16[32,32,256]{2,1,0:T(8,128)(2,1)}), bf16[32,32,256]{2,1,0:T(8,128)(2,1)}, u32[]{:S(2)}, u32[]{:S(2)}) async-start(bf16[32,32,256]{2,1,0:T(8,128)(2,1)} %pad_maximum_fusion), calls=%async_computation | async-start | bytes 1048576 | tf_op jit(solution)/shard_map/all_to_all | solution.py:25
  67.3 17.1 %copy-start.10 = (bf16[1,1,1,16,1536]{4,3,2,1,0:T(8,128)(2,1)S(1)}, bf16[1,1,1,16,1536]{4,3,2,1,0:T(8,128)(2,1)}, u32[]{:S(2)}) copy-start(bf16[1,1,1,16,1536]{4,3,2,1,0:T(8,128)(2,1)} %param.16) | copy-start | bytes 147460
  67.3 5.8 %collective-permute-start.5 = (bf16[32,2048]{1,0:T(8,128)(2,1)S(1)}, bf16[32,2048]{1,0:T(8,128)(2,1)S(1)}, u32[]{:S(2)}, u32[]{:S(2)}) collective-permute-start(bf16[32,2048]{1,0:T(8,128)(2,1)S(1)} %reduce_sum.61), channel_id=1, source_target_pairs={{0,32},{32,0},{1,33},{33,1},{2,34},{34,2},{3,35},{35,3},{4,36},{36... | collective-permute-start | bytes 393224 | tf_op jit(solution)/shard_map/ppermute | solution.py:21
  76.1 12.3 %all-to-all-start.3 = ((bf16[8,8,256]{2,1,0:T(8,128)(2,1)}), bf16[8,8,256]{2,1,0:T(8,128)(2,1)S(1)}, u32[]{:S(2)}, u32[]{:S(2)}) async-start(bf16[8,8,256]{2,1,0:T(8,128)(2,1)} %fusion.40), calls=%async_computation.3 | async-start | bytes 65536 | tf_op jit(solution)/shard_map/all_to_all | solution.py:25
  95.0 5.4 %copy-start.4 = (bf16[256,1536]{0,1:T(8,128)(2,1)}, bf16[256,1536]{0,1:T(8,128)(2,1)S(1)}, u32[]{:S(2)}) copy-start(bf16[256,1536]{0,1:T(8,128)(2,1)S(1)} %fusion.13) | copy-start | bytes 2359300
  97.1 13.9 %collective-permute-start.10 = (bf16[512,256]{1,0:T(8,128)(2,1)S(1)}, bf16[512,256]{1,0:T(8,128)(2,1)S(1)}, u32[]{:S(2)}, u32[]{:S(2)}) collective-permute-start(bf16[512,256]{1,0:T(8,128)(2,1)S(1)} %fusion.36), channel_id=1, source_target_pairs={{0,32},{32,0},{1,33},{33,1},{2,34},{34,2},{3,35},{35,3},{4,36},{36... | collective-permute-start | bytes 786440 | tf_op jit(solution)/shard_map/ppermute | solution.py:21
  98.5 11.1 %collective-permute-start.6 = (bf16[256,256]{1,0:T(8,128)(2,1)S(1)}, bf16[256,256]{1,0:T(8,128)(2,1)S(1)}, u32[]{:S(2)}, u32[]{:S(2)}) collective-permute-start(bf16[256,256]{1,0:T(8,128)(2,1)S(1)} %get-tuple-element.13), channel_id=1, source_target_pairs={{0,32},{32,64},{64,96},{96,128},{128,160},{160,192},{192,224},{1,3... | collective-permute-start | bytes 393224 | tf_op jit(solution)/shard_map/ppermute | solution.py:17
  100.6 21.6 %collective-permute-start.9 = (bf16[256,256]{1,0:T(8,128)(2,1)}, bf16[256,256]{1,0:T(8,128)(2,1)}, u32[]{:S(2)}, u32[]{:S(2)}) collective-permute-start(bf16[256,256]{1,0:T(8,128)(2,1)} %get-tuple-element.10), channel_id=1, source_target_pairs={{8,0},{16,8},{24,16},{9,1},{17,9},{25,17},{10,2},{18,10},{26,18},{... | collective-permute-start | bytes 393224 | tf_op jit(solution)/shard_map/ppermute | solution.py:17
  101.9 18.1 %collective-permute-start.8 = (bf16[256,256]{1,0:T(8,128)(2,1)}, bf16[256,256]{1,0:T(8,128)(2,1)}, u32[]{:S(2)}, u32[]{:S(2)}) collective-permute-start(bf16[256,256]{1,0:T(8,128)(2,1)} %get-tuple-element.11), channel_id=1, source_target_pairs={{0,8},{8,16},{16,24},{1,9},{9,17},{17,25},{2,10},{10,18},{18,26},{... | collective-permute-start | bytes 393224 | tf_op jit(solution)/shard_map/ppermute | solution.py:17
  106.6 11.2 %collective-permute-start.7 = (bf16[256,256]{1,0:T(8,128)(2,1)}, bf16[256,256]{1,0:T(8,128)(2,1)}, u32[]{:S(2)}, u32[]{:S(2)}) collective-permute-start(bf16[256,256]{1,0:T(8,128)(2,1)} %get-tuple-element.12), channel_id=1, source_target_pairs={{32,0},{64,32},{96,64},{128,96},{160,128},{192,160},{224,192},{33,... | collective-permute-start | bytes 393224 | tf_op jit(solution)/shard_map/ppermute | solution.py:17
  112.3 17.2 %all-to-all-start.4 = ((bf16[32,24,256]{2,1,0:T(8,128)(2,1)}), bf16[32,24,256]{2,1,0:T(8,128)(2,1)S(1)}, u32[]{:S(2)}, u32[]{:S(2)}) async-start(bf16[32,24,256]{2,1,0:T(8,128)(2,1)} %pad_maximum_fusion.1), calls=%async_computation.4 | async-start | bytes 786432 | tf_op jit(solution)/shard_map/all_to_all | solution.py:25
  131.0 12.4 %all-to-all-start.5 = ((bf16[8,8,256]{2,1,0:T(8,128)(2,1)}), bf16[8,8,256]{2,1,0:T(8,128)(2,1)}, u32[]{:S(2)}, u32[]{:S(2)}) async-start(bf16[8,8,256]{2,1,0:T(8,128)(2,1)} %fusion.41), calls=%async_computation.5 | async-start | bytes 65536 | tf_op jit(solution)/shard_map/all_to_all | solution.py:25
  138.4 5.8 %copy-start.9 = (bf16[1,1,1,8,1536]{4,3,2,1,0:T(8,128)(2,1)S(1)}, bf16[1,1,1,8,1536]{4,3,2,1,0:T(8,128)(2,1)}, u32[]{:S(2)}) copy-start(bf16[1,1,1,8,1536]{4,3,2,1,0:T(8,128)(2,1)} %param.17) | copy-start | bytes 73732
  (9 other events, 12.9 us)

commit v2 on v1

v2 whole, which is shorter than its diff:
```python
import functools

import jax
import jax.numpy as jnp
from jax import lax
from jax.experimental import pallas as pl
from jax.experimental.pallas import tpu as pltpu
from jax.sharding import Mesh
from jax.sharding import PartitionSpec as P

ITERS = 2
RADIX_BITS = 6
RADIX = 1 << RADIX_BITS
LANES = 128
GRID = ("y", "core")
BULK = ("y", "z")
LINE = ("core", "x")
SOLVE_PARTS = 3
FAR_PARTS = 2
LIMIT = 32 * 1024 * 1024

VMEM = pl.BlockSpec(memory_space=pltpu.VMEM)
HBM = pl.BlockSpec(memory_space=pltpu.HBM)
DMA = pltpu.SemaphoreType.DMA


def paired(block, axis, pairs):
    route = [(a, b) for a, b in pairs] + [(b, a) for a, b in pairs]
    return lax.ppermute(block, axis, route)


def turned(block, axis, distance):
    size = lax.axis_size(axis)
    return lax.ppermute(block, axis, [(i, (i + distance) % size) for i in range(size)])


def summed(block, axis):
    others = [turned(block, axis, distance) for distance in range(1, lax.axis_size(axis))]
    for other in others:
        block = block + other
    return block


def exchanged(block, axis):
    return lax.all_to_all(block, axis, split_axis=0, concat_axis=0, tiled=True)


def product(left, right, dims=((1,), (0,))):
    return lax.dot_general(left, right, (dims, ((), ())), preferred_element_type=jnp.float32)


def called(kernel, name, ins, outs, args, scratch=()):
    args = [
        pltpu.with_memory_space_constraint(arg, pltpu.HBM) if spec is HBM else arg
        for arg, spec in zip(args, ins)
    ]
    shapes = [pltpu.HBM(out.shape, out.dtype) if spec is HBM else out for out, spec in outs]
    return pl.pallas_call(
        kernel,
        out_shape=tuple(shapes),
        in_specs=ins,
        out_specs=tuple(spec for _, spec in outs),
        scratch_shapes=list(scratch),
        compiler_params=pltpu.CompilerParams(vmem_limit_bytes=LIMIT),
        name=name,
    )(*args)


def moved(source, target, sem):
    copy = pltpu.make_async_copy(source, target, sem)
    copy.start()
    return copy


def moved_parts(source, target, sems, parts):
    rows = source.shape[0] // parts
    copies = []
    for part in range(parts):
        where = pl.ds(part * rows, rows)
        copies.append(moved(source.at[where], target.at[where], sems.at[part]))
    return copies


def write_ids(ids_ref, slots_ref, rows_ref):
    count, columns = rows_ref.shape
    half = columns // 2
    sub = lax.broadcasted_iota(jnp.int32, (count, half), 0)
    high = jnp.zeros((count, half), jnp.int32)
    low = jnp.zeros((count, half), jnp.int32)
    for q in range(count):
        value = ids_ref[0, q]
        high = jnp.where(sub == q, value >> RADIX_BITS, high)
        low = jnp.where(sub == q, value & (RADIX - 1), low)
    rows = jnp.concatenate([high, low], axis=1).astype(jnp.float32).astype(jnp.bfloat16)
    rows_ref[...] = rows
    slots_ref[...] = jnp.zeros(slots_ref.shape, slots_ref.dtype)
    slots_ref[lax.axis_index("x")] = rows


def read_ids(rows):
    half = rows.shape[1] // 2
    return rows[:, :half] * float(RADIX) + rows[:, half:]


def hot_rows(ids, count, start):
    lane = lax.broadcasted_iota(jnp.int32, (1, LANES), 1).astype(jnp.float32)
    parts = []
    for block in range(count // LANES):
        local = ids - (start + float(block * LANES))
        parts.append((local == lane).astype(jnp.float32).astype(jnp.bfloat16))
    return jnp.concatenate(parts, axis=1)


def rows_kernel(slots_ref, coarse_ref, held_ref, coarse, sem):
    copy = moved(coarse_ref, coarse, sem)
    own = coarse_ref.shape[0]
    line, count, columns = slots_ref.shape
    rows = slots_ref[...].astype(jnp.float32).reshape(line * count, columns)
    start = (lax.axis_index("x") * own).astype(jnp.float32)
    hot = hot_rows(read_ids(rows), own, start)
    copy.wait()
    held_ref[...] = product(hot, coarse[...]).astype(jnp.bfloat16)


def routes(core, targets, ranks, route, shape):
    bulk, depth_bits, limit = shape
    entries = targets.shape[1]
    spots = entries * limit
    side = ((targets >> depth_bits) & 1) ^ core
    low = targets & ((1 << depth_bits) - 1)
    places = side * bulk + ((targets >> (depth_bits + 1)) << depth_bits) + low
    owner = lax.broadcasted_iota(jnp.int32, (entries, spots), 1) // limit
    entry = lax.broadcasted_iota(jnp.int32, (entries, spots), 0)
    widen = (owner == entry).astype(jnp.float32).astype(jnp.bfloat16)

    def spread(values):
        wide = jnp.broadcast_to(values.astype(jnp.float32), (limit, entries))
        return product(wide.astype(jnp.bfloat16), widen)

    row = lax.broadcasted_iota(jnp.int32, (limit, spots), 0).astype(jnp.float32)
    column = (lax.broadcasted_iota(jnp.int32, (limit, spots), 1) % limit).astype(jnp.float32)
    live = jnp.logical_and(row == column, row < spread(ranks))
    keys = jnp.where(live, spread(places), -1.0)
    for place in range(entries):
        hit = (keys == float(place)).astype(jnp.float32).astype(jnp.bfloat16)
        route[pl.ds(place * limit, limit), :] = hit


def corrected(base, corners, shares):
    picked = jnp.sum(shares.astype(jnp.float32), axis=0).astype(jnp.bfloat16)
    return base - product(corners, picked, ((0,), (0,)))


def solve_kernel(first, shape, *refs):
    targets_hbm, ranks_hbm, corners_hbm, inverse_hbm, bases_hbm = refs[:5]
    if first:
        source_hbm, ids_hbm, refs = refs[5], refs[6], refs[7:]
    else:
        base_hbm, shares_ref, refs = refs[5], refs[6], refs[7:]
    swap_ref, kept_ref, terms_ref, solved_hbm, grid_hbm, even_hbm, odd_hbm = refs[:7]
    refs = refs[7:]
    if first:
        slots_ref, id_rows_ref, refs = refs[0], refs[1], refs[2:]
    else:
        whole_hbm, refs = refs[0], refs[1:]
    targets, ranks, corners, inverse, bases, route, coefficient, solved_ref = refs[:8]
    sems, inverse_sems, bases_sems, refs = refs[8], refs[9], refs[10], refs[11:]
    core = lax.axis_index("core")
    odd = lax.axis_index("x") & 1
    face = grid_hbm.shape[0]
    half = kept_ref.shape[0]

    tables = [moved(targets_hbm, targets, sems.at[0]), moved(ranks_hbm, ranks, sems.at[1])]
    if first:
        source, ids = refs
        inputs = [moved(source_hbm, source, sems.at[2])]
        ids_copy = moved(ids_hbm, ids, sems.at[3])
    else:
        base, whole_ref = refs
        inputs = [moved(base_hbm, base, sems.at[2])]
    corner_copy = moved(corners_hbm, corners, sems.at[4])
    inverse_copies = moved_parts(inverse_hbm, inverse, inverse_sems, SOLVE_PARTS)
    bases_copies = moved_parts(bases_hbm, bases, bases_sems, FAR_PARTS)
    leaving = []
    for copy in tables:
        copy.wait()
    routes(core, targets[...], ranks[...], route, shape)
    if first:
        ids_copy.wait()
        write_ids(ids, slots_ref, id_rows_ref)
    corner_copy.wait()
    for copy in inputs:
        copy.wait()
    if first:
        rounded = source[...]
    else:
        whole = corrected(base[...], corners[...], shares_ref[...])
        whole_ref[...] = whole
        leaving.append(moved(whole_ref, whole_hbm, sems.at[5]))
        rounded = whole.astype(jnp.bfloat16)
    rows = inverse.shape[0] // SOLVE_PARTS
    for part, copy in enumerate(inverse_copies):
        copy.wait()
        where = pl.ds(part * rows, rows)
        solved_ref[where, :] = product(inverse[where, :], rounded).astype(jnp.bfloat16)
    leaving.append(moved(solved_ref, solved_hbm, sems.at[6]))

    def part_of(index):
        return solved_ref.at[pl.ds(pl.multiple_of(index * face, face), face)]

    leaving.append(moved(part_of(core), grid_hbm, sems.at[7]))
    leaving.append(moved(part_of(3 - odd), even_hbm, sems.at[8]))
    leaving.append(moved(part_of(2 + odd), odd_hbm, sems.at[9]))
    solved = solved_ref[...]
    rows = bases.shape[0] // FAR_PARTS
    for part, copy in enumerate(bases_copies):
        copy.wait()
        where = pl.ds(part * rows, rows)
        coefficient[where, :] = product(bases[where, :], solved).astype(jnp.bfloat16)
    terms_ref[...] = product(corners[...], solved).astype(jnp.bfloat16)
    values = coefficient[...]
    swap_ref[:half] = product(route[half:], values).astype(jnp.bfloat16)
    swap_ref[half:] = part_of(1 - core)[...]
    kept_ref[...] = product(route[:half], values)
    for copy in leaving:
        copy.wait()


def pack_kernel(count, *refs):
    kept_ref, swapped_ref, extras = refs[0], refs[1], refs[2:-3]
    payload_ref, face_hbm, sem = refs[-3:]
    bulk, _, columns = payload_ref.shape
    half = kept_ref.shape[0]
    copy = moved(swapped_ref.at[pl.ds(half, face_hbm.shape[0])], face_hbm, sem)
    total = kept_ref[...] + swapped_ref[:half].astype(jnp.float32)
    limit = half // bulk
    payload_ref[:, :limit] = total.reshape(bulk, limit, columns).astype(jnp.bfloat16)
    for number, extra in enumerate(extras):
        wide = jnp.broadcast_to(extra[...].astype(jnp.float32)[None], (bulk, count, columns))
        start = limit + number * count
        payload_ref[:, start : start + count] = wide.astype(jnp.bfloat16)
    copy.wait()


def middle_kernel(first, limit, count, *refs):
    if first:
        landed_ref, own_ref, other_ref, partial_ref, arrived_hbm, coupling_hbm = refs[:6]
        arrived_ref, coupling_ref, sems = refs[6:]
    else:
        landed_ref, coupling_ref, partial_ref, arrived_hbm, arrived_ref, sems = refs
    bulk, _, columns = landed_ref.shape

    def slab(number):
        start = limit + number * count
        block = landed_ref[:, start : start + count].astype(jnp.float32)
        return block.reshape(bulk * count, columns)

    terms = slab(0).astype(jnp.bfloat16)
    line = partial_ref.shape[0] // 2
    leaving = []
    if first:
        placed = hot_rows(read_ids(slab(1)), own_ref.shape[1], 0.0)
        for number, rows_ref in enumerate((own_ref, other_ref)):
            coupling = product(rows_ref[...], placed, ((1,), (1,)))
            coupling_ref[number] = coupling.astype(jnp.bfloat16)
        leaving.append(moved(coupling_ref, coupling_hbm, sems.at[0]))
    core = lax.axis_index("core")
    for number, start in enumerate((core * line, (1 - core) * line)):
        partial = product(coupling_ref[number], terms).reshape(line, count, columns)
        partial_ref[pl.ds(start, line)] = partial.astype(jnp.bfloat16)
    arrived = jnp.sum(landed_ref[:, :limit].astype(jnp.float32), axis=0)
    arrived_ref[...] = arrived.astype(jnp.bfloat16)
    leaving.append(moved(arrived_ref, arrived_hbm, sems.at[1]))
    for copy in leaving:
        copy.wait()


def update_kernel(*refs):
    count = (len(refs) - 6) // 2
    sources, (grid, even, odd_face), base_hbm = refs[:count], refs[count : count + 3], refs[count + 3]
    targets, (base_ref, sems) = refs[count + 4 : 2 * count + 4], refs[2 * count + 4 :]
    copies = [moved(a, b, sems.at[i]) for i, (a, b) in enumerate(zip(sources, targets))]
    for copy in copies:
        copy.wait()
    links, patch, arrived, source, whole, solved, swapped = targets
    core = lax.axis_index("core")
    odd = lax.axis_index("x") & 1
    face = grid.shape[0]
    far = product(patch[...], arrived[...], ((0,), (0,)))
    known = whole[...].astype(jnp.float32) + source[...].astype(jnp.float32)
    base_ref[...] = known - solved[...].astype(jnp.float32) - far
    for index, block in ((1 - core, swapped), (core, grid), (3 - odd, even), (2 + odd, odd_face)):
        where = pl.ds(pl.multiple_of(index * face, face), face)
        link = links[0, index].astype(jnp.float32)
        base_ref[where, :] = base_ref[where, :] + block[...].astype(jnp.float32) * link
    last = moved(base_ref, base_hbm, sems.at[count])
    last.wait()


def final_kernel(base_hbm, shares_ref, corners_hbm, inverse_hbm, whole_hbm, field_hbm, *scratch):
    base, corners, inverse, whole_ref, field_ref, sems, inverse_sems, field_sems = scratch
    inputs = [
        moved(base_hbm, base, sems.at[0]),
        moved(corners_hbm, corners, sems.at[2]),
    ]
    copies = moved_parts(inverse_hbm, inverse, inverse_sems, SOLVE_PARTS)
    for copy in inputs:
        copy.wait()
    whole = corrected(base[...], corners[...], shares_ref[...])
    whole_ref[...] = whole
    leaving = [moved(whole_ref, whole_hbm, sems.at[3])]
    rounded = whole.astype(jnp.bfloat16)
    rows = inverse.shape[0] // SOLVE_PARTS
    for part, copy in enumerate(copies):
        copy.wait()
        where = pl.ds(part * rows, rows)
        field_ref[where, :] = product(inverse[where, :], rounded).astype(jnp.bfloat16)
        leaving.append(moved(field_ref.at[where], field_hbm.at[where], field_sems.at[part]))
    for copy in leaving:
        copy.wait()


def body(
    right_side,
    interface_inverse,
    face_link,
    far_target,
    far_rank,
    far_basis,
    patch_basis,
    corner_basis,
    corner_row,
    coarse_inverse,
):
    bf16, f32, i32 = jnp.bfloat16, jnp.float32, jnp.int32
    order = interface_inverse.shape[-1]
    columns = right_side.shape[-1]
    face = order // 6
    inverse = interface_inverse.reshape(order, order)
    source = right_side.reshape(order, columns)
    links = face_link.reshape(1, -1)
    limit = far_basis.shape[-2]
    bases = far_basis.reshape(-1, order)
    patch = patch_basis.reshape(limit, order)
    corners = corner_basis.reshape(-1, order)
    count = corners.shape[0]
    ids = corner_row.reshape(1, -1)
    own_coarse, coarse_order = coarse_inverse.shape
    targets = far_target.reshape(1, -1)
    ranks = far_rank.reshape(1, -1)
    entries = targets.shape[1]
    depth = lax.axis_size("z")
    bulk = lax.axis_size("y") * depth
    line = lax.axis_size("x")
    spots = bases.shape[0]
    half = spots // 2
    shape = (bulk, depth.bit_length() - 1, limit)
    struct = jax.ShapeDtypeStruct
    near = [(i, i + 1) for i in range(0, line, 2)]
    apart = [(i, i + 1) for i in range(1, line - 1, 2)]
    between = [(i, i + 1) for i in range(1, 2 * lax.axis_size("y") - 1, 2)]

    whole = source
    base = shares = coupling = None
    for sweep in range(ITERS):
        initial = sweep == 0
        outs = [
            (struct((half + face, columns), bf16), VMEM),
            (struct((half, columns), f32), VMEM),
            (struct((count, columns), bf16), VMEM),
            (struct((order, columns), bf16), HBM),
        ] + [(struct((face, columns), bf16), HBM)] * 3
        args = [targets, ranks, corners, inverse, bases]
        scratch = [
            pltpu.VMEM((1, entries), i32),
            pltpu.VMEM((1, entries), i32),
            pltpu.VMEM((count, order), bf16),
            pltpu.VMEM((order, order), bf16),
            pltpu.VMEM((spots, order), bf16),
            pltpu.VMEM((spots, spots), bf16),
            pltpu.VMEM((spots, columns), bf16),
            pltpu.VMEM((order, columns), bf16),
            DMA((10,)),
            DMA((SOLVE_PARTS,)),
            DMA((FAR_PARTS,)),
        ]
        if initial:
            args += [source, ids]
            outs += [
                (struct((line, count, columns), bf16), VMEM),
                (struct((count, columns), bf16), VMEM),
            ]
            scratch += [pltpu.VMEM((order, columns), bf16), pltpu.SMEM((1, count), i32)]
        else:
            args += [base, shares]
            outs += [(struct((order, columns), f32), HBM)]
            scratch += [pltpu.VMEM((order, columns), f32)] * 2
        results = called(
            functools.partial(solve_kernel, initial, shape),
            "solve",
            [HBM] * 6 + [HBM if initial else VMEM],
            outs,
            args,
            scratch,
        )
        swap, kept, terms, solved, to_grid, to_even, to_odd = results[:7]
        extras = [terms]
        if initial:
            slots, id_rows = results[7:]
            extras += [id_rows]
            slots = summed(slots, "x")
        else:
            whole = results[7]
        swapped = paired(swap, "core", [(0, 1)])
        payload, from_core = called(
            functools.partial(pack_kernel, count),
            "pack",
            [VMEM] * (2 + len(extras)),
            [
                (struct((bulk, limit + count * len(extras), columns), bf16), VMEM),
                (struct((face, columns), bf16), HBM),
            ],
            [kept, swapped] + extras,
            [DMA],
        )
        landed = exchanged(payload, BULK)
        if initial:
            (held,) = called(
                rows_kernel,
                "rows",
                [VMEM, HBM],
                [(struct((line * count, coarse_order), bf16), VMEM)],
                (slots, coarse_inverse),
                [pltpu.VMEM((own_coarse, coarse_order), bf16), DMA],
            )
            own_rows = summed(held, "x")
            other_rows = paired(own_rows, "core", [(0, 1)])
        from_grid = paired(to_grid, GRID, between)
        from_even = paired(to_even, "x", near)
        from_odd = paired(to_odd, "x", apart)
        args = [landed] + ([own_rows, other_rows] if initial else [coupling])
        outs = [
            (struct((2 * line, count, columns), bf16), VMEM),
            (struct((limit, columns), bf16), HBM),
        ]
        scratch = [pltpu.VMEM((limit, columns), bf16)]
        if initial:
            outs += [(struct((2, line * count, bulk * count), bf16), HBM)]
            scratch += [pltpu.VMEM((2, line * count, bulk * count), bf16)]
        results = called(
            functools.partial(middle_kernel, initial, limit, count),
            "middle",
            [VMEM] * len(args),
            outs,
            args,
            scratch + [DMA((2,))],
        )
        partial, arrived = results[:2]
        if initial:
            coupling = results[2]
        shares = exchanged(partial, LINE)
        args = [links, patch, arrived, source, whole, solved, from_core]
        (base,) = called(
            update_kernel,
            "update",
            [HBM] * len(args) + [VMEM] * 3,
            [(struct((order, columns), f32), HBM)],
            args + [from_grid, from_even, from_odd],
            [pltpu.SMEM(links.shape, i32)]
            + [pltpu.VMEM(arg.shape, arg.dtype) for arg in args[1:]]
            + [pltpu.VMEM((order, columns), f32), DMA((len(args) + 1,))],
        )
    whole, field = called(
        final_kernel,
        "final",
        [HBM, VMEM, HBM, HBM],
        [(struct((order, columns), f32), HBM), (struct((order, columns), bf16), HBM)],
        (base, shares, corners, inverse),
        [
            pltpu.VMEM((order, columns), f32),
            pltpu.VMEM((count, order), bf16),
            pltpu.VMEM((order, order), bf16),
            pltpu.VMEM((order, columns), f32),
            pltpu.VMEM((order, columns), bf16),
            DMA((4,)),
            DMA((SOLVE_PARTS,)),
            DMA((SOLVE_PARTS,)),
        ],
    )
    return whole.reshape(right_side.shape), field.reshape(right_side.shape)


def solution(mesh):
    sizes = mesh.shape
    fine = Mesh(
        mesh.devices.reshape(sizes["sx"] // 2, 2, sizes["sy"], sizes["sz"]), ("y", "core", "x", "z")
    )
    sub = P(GRID, "x", "z")
    return jax.shard_map(
        body,
        mesh=fine,
        in_specs=(sub,) * 9 + (P("x", None),),
        out_specs=(sub, sub),
        check_vma=False,
    )
```

time: 156 us -> 114 us (0.73); the launches traced: 154 us -> 114 us
  Pallas kernels: 0 us -> 38.8 us
  matrix products: 37 us -> 0 us
  other arithmetic: 22.8 us -> 0.04 us
  starting transfers between devices: 66 us -> 53.8 us
  local copies, waits for them, and re-layouts: 12.2 us -> 0.03 us
  waiting for transfers between devices: 15.1 us -> 20 us
    pallas_call x0 -> x10, Pallas kernels: none -> 38.8 us  [called(): pl.pallas_call(kernel, out_shape=tuple(shapes), in_specs=ins, out_specs=t...]
    dot_general x19 -> x0, matrix products: 37 us -> none  [product(): lax.dot_general(left, right, (dims, ((), ())), preferred_element_type=jnp...]
    unnamed x8 -> x0, other arithmetic: 15.3 us -> none
    ppermute x11 -> x15, waiting for transfers between devices: 0.03 us -> 11.2 us  [the longest x6 8.53 us: turned(): lax.ppermute(block, axis, [(i, (i + distance) % size) for i in range(size)])]
    all_to_all x6 -> x4, starting transfers between devices: 40.5 us -> 31.4 us  [exchanged(): return lax.all_to_all(block, axis, split_axis=0, concat_axis=0, tiled=True)]
    unnamed x33 -> x14, local copies, waits for them, and re-layouts: 6.57 us -> 0.03 us
    all_to_all x6 -> x4, waiting for transfers between devices: 15.1 us -> 8.79 us  [exchanged(): return lax.all_to_all(block, axis, split_axis=0, concat_axis=0, tiled=True)]
    ppermute x11 -> x15, starting transfers between devices: 25.5 us -> 22.4 us  [the longest x9 16.2 us: paired(): return lax.ppermute(block, axis, route)]
  transfers between devices with their start and end apart: 17 -> 19, of which waited for: 5 -> 10; matrix products, arithmetic and copies ran while one was open for 30% -> 0% of each run, Pallas kernels for 0% -> 11%
where the time goes in v2:
time: 114 us
  starting transfers between devices  53.8 us (47%)
  Pallas kernels  38.8 us (34%)
  waiting for transfers between devices  20 us (18%)
    pallas_call x10, Pallas kernels, called(): pl.pallas_call(kernel, out_shape=tuple(shapes), in_specs=ins, out_specs=t...  38.8 us
    all_to_all x4, starting transfers between devices, exchanged(): return lax.all_to_all(block, axis, split_axis=0, concat_axis=0, tiled=True)  31.4 us
    ppermute x9, starting transfers between devices, paired(): return lax.ppermute(block, axis, route)  16.2 us
    all_to_all x4, waiting for transfers between devices, exchanged(): return lax.all_to_all(block, axis, split_axis=0, concat_axis=0, tiled=True)  8.79 us
    ppermute x6, waiting for transfers between devices, turned(): lax.ppermute(block, axis, [(i, (i + distance) % size) for i in range(size)])  8.53 us
    ppermute x6, starting transfers between devices, turned(): lax.ppermute(block, axis, [(i, (i + distance) % size) for i in range(size)])  6.15 us
    ppermute x9, waiting for transfers between devices, paired(): return lax.ppermute(block, axis, route)  2.72 us
  transfers between devices with their start and end apart: 19, of which 10 were waited for; matrix products, arithmetic and copies ran while one was open for 0% of the time, Pallas kernels for 11%

profile of v2, /device:TPU:1, one launch (start us, length us, event | category | flops | bytes accessed | tf_op | source)
XLA Modules:
  0.0 113.8 jit_solution(8963072948507696423)
XLA Ops:
  0.6 8.1 %solve.2 = (bf16[768,256]{1,0:T(8,128)(2,1)S(1)}, f32[512,256]{1,0:T(8,128)S(1)}, bf16[8,256]{1,0:T(8,128)(2,1)S(1)}, bf16[1536,256]{1,0:T(8,128)(2,1)}, bf16[25...) custom-call(s32[1,64]{1,0:T(1,128)} %bitcast.25, ...), custom_call_target="tpu_custom_call" | custom-call | tf_op jit(solution)/shard_map/solve/pallas_call | solution.py:58
  8.7 3.3 %collective-permute-start = (bf16[768,256]{1,0:T(8,128)(2,1)S(1)}, bf16[768,256]{1,0:T(8,128)(2,1)S(1)}, u32[]{:S(2)}, u32[]{:S(2)}) collective-permute-start(bf16[768,256]{1,0:T(8,128)(2,1)S(1)} %get-tuple-element.31), channel_id=1, source_target_pairs={{0,32},{32,0},{1,33},{33,1},{2,34},{34,2},{3,35},{35,3},{4,36},{36... | collective-permute-start | bytes 1179656 | tf_op jit(solution)/shard_map/ppermute | solution.py:29
  12.0 1.3 %collective-permute-done.refs_1_ = bf16[768,256]{1,0:T(8,128)(2,1)S(1)} collective-permute-done((bf16[768,256]{1,0:T(8,128)(2,1)S(1)}, bf16[768,256]{1,0:T(8,128)(2,1)S(1)}, u32[]{:S(2)}, u32[]{:S(2)}) %collective-permute-start) | collective-permute-done | bytes 393248 | tf_op jit(solution)/shard_map/ppermute | solution.py:29
  13.3 1.4 %pack.2 = (bf16[32,32,256]{2,1,0:T(8,128)(2,1)}, bf16[256,256]{1,0:T(8,128)(2,1)}) custom-call(f32[512,256]{1,0:T(8,128)S(1)} %get-tuple-element.30.refs_0_, bf16[768,256]{1,0:T(8,128)(2,1)S(1)} %collective-permute-done.refs_1_, bf16[8,256]{1,0:T(8,128)(2,1)S(1)} %get-tuple-element.32.refs_2_, bf16[8,256]{1,0:T(8,128)(2,1)S(1)} %get-tuple-element.33.refs_3_), custom_call_target="tpu_custom_call" | custom-call | tf_op jit(solution)/shard_map/pack/pallas_call | solution.py:58
  14.8 9.5 %all-to-all-start = ((bf16[32,32,256]{2,1,0:T(8,128)(2,1)}), bf16[32,32,256]{2,1,0:T(8,128)(2,1)S(1)}, u32[]{:S(2)}, u32[]{:S(2)}) async-start(bf16[32,32,256]{2,1,0:T(8,128)(2,1)} %get-tuple-element.34), calls=%async_computation | async-start | bytes 1048576 | tf_op jit(solution)/shard_map/all_to_all | solution.py:45
  24.3 2.6 %collective-permute-start.3 = (bf16[4,8,256]{2,1,0:T(8,128)(2,1)S(1)}, bf16[4,8,256]{2,1,0:T(8,128)(2,1)S(1)}, u32[]{:S(2)}, u32[]{:S(2)}) collective-permute-start(bf16[4,8,256]{2,1,0:T(8,128)(2,1)S(1)} %get-tuple-element.35), channel_id=1, source_target_pairs={{0,24},{8,0},{16,8},{24,16},{1,25},{9,1},{17,9},{25,17},{2,26},{10... | collective-permute-start | bytes 49160 | tf_op jit(solution)/shard_map/ppermute | solution.py:34
  28.0 3.0 %collective-permute-done.2 = bf16[4,8,256]{2,1,0:T(8,128)(2,1)S(1)} collective-permute-done((bf16[4,8,256]{2,1,0:T(8,128)(2,1)S(1)}, bf16[4,8,256]{2,1,0:T(8,128)(2,1)S(1)}, u32[]{:S(2)}, u32[]{:S(2)}) %collective-permute-start.2) | collective-permute-done | bytes 16416 | tf_op jit(solution)/shard_map/ppermute | solution.py:34
  31.2 2.1 %rows.1 = bf16[32,2048]{1,0:T(8,128)(2,1)S(1)} custom-call(bf16[4,8,256]{2,1,0:T(8,128)(2,1)S(1)} %add_add_fusion.1.slots_ref, bf16[512,2048]{1,0:T(8,128)(2,1)} %coarse_ref.1), custom_call_target="tpu_custom_call" | custom-call | tf_op jit(solution)/shard_map/rows/pallas_call | solution.py:58
  35.8 1.7 %collective-permute-done.6 = bf16[32,2048]{1,0:T(8,128)(2,1)S(1)} collective-permute-done((bf16[32,2048]{1,0:T(8,128)(2,1)S(1)}, bf16[32,2048]{1,0:T(8,128)(2,1)S(1)}, u32[]{:S(2)}, u32[]{:S(2)}) %collective-permute-start.6) | collective-permute-done | bytes 131104 | tf_op jit(solution)/shard_map/ppermute | solution.py:34
  37.5 2.0 %collective-permute-done.5 = bf16[32,2048]{1,0:T(8,128)(2,1)S(1)} collective-permute-done((bf16[32,2048]{1,0:T(8,128)(2,1)S(1)}, bf16[32,2048]{1,0:T(8,128)(2,1)S(1)}, u32[]{:S(2)}, u32[]{:S(2)}) %collective-permute-start.5) | collective-permute-done | bytes 131104 | tf_op jit(solution)/shard_map/ppermute | solution.py:34
  39.5 1.6 %collective-permute-done.4 = bf16[32,2048]{1,0:T(8,128)(2,1)S(1)} collective-permute-done((bf16[32,2048]{1,0:T(8,128)(2,1)S(1)}, bf16[32,2048]{1,0:T(8,128)(2,1)S(1)}, u32[]{:S(2)}, u32[]{:S(2)}) %collective-permute-start.4) | collective-permute-done | bytes 131104 | tf_op jit(solution)/shard_map/ppermute | solution.py:34
  41.1 3.2 %collective-permute-start.7 = (bf16[32,2048]{1,0:T(8,128)(2,1)S(1)}, bf16[32,2048]{1,0:T(8,128)(2,1)S(1)}, u32[]{:S(2)}, u32[]{:S(2)}) collective-permute-start(bf16[32,2048]{1,0:T(8,128)(2,1)S(1)} %add_add_fusion.refs_1_), channel_id=1, source_target_pairs={{0,32},{32,0},{1,33},{33,1},{2,34},{34,2},{3,35},{35,3},{4,36},{36... | collective-permute-start | bytes 393224 | tf_op jit(solution)/shard_map/ppermute | solution.py:29
  44.4 3.3 %collective-permute-start.8 = (bf16[256,256]{1,0:T(8,128)(2,1)S(1)}, bf16[256,256]{1,0:T(8,128)(2,1)S(1)}, u32[]{:S(2)}, u32[]{:S(2)}) collective-permute-start(bf16[256,256]{1,0:T(8,128)(2,1)S(1)} %copy-done.3), channel_id=1, source_target_pairs={{32,64},{96,128},{160,192},{64,32},{128,96},{192,160},{33,65},{97,... | collective-permute-start | bytes 393224 | tf_op jit(solution)/shard_map/ppermute | solution.py:29
  48.6 2.0 %middle.2 = (bf16[8,8,256]{2,1,0:T(8,128)(2,1)}, bf16[16,256]{1,0:T(8,128)(2,1)}, bf16[2,32,256]{2,1,0:T(8,128)(2,1)}) custom-call(bf16[32,32,256]{2,1,0:T(8,128)(2,1)S(1)} %all-to-all-done.refs_0_, bf16[32,2048]{1,0:T(8,128)(2,1)S(1)} %add_add_fusion.refs_1_, bf16[32,2048]{1,0:T(8,128)(2,1)S(1)} %collective-permute-done.7.refs_2_), custom_call_target="tpu_custom_call" | custom-call | tf_op jit(solution)/shard_map/middle/pallas_call | solution.py:58
  50.6 6.1 %all-to-all-start.1 = ((bf16[8,8,256]{2,1,0:T(8,128)(2,1)}), bf16[8,8,256]{2,1,0:T(8,128)(2,1)S(1)}, u32[]{:S(2)}, u32[]{:S(2)}) async-start(bf16[8,8,256]{2,1,0:T(8,128)(2,1)} %get-tuple-element.42), calls=%async_computation.1 | async-start | bytes 65536 | tf_op jit(solution)/shard_map/all_to_all | solution.py:45
  56.7 3.8 %update.2.refs_5_ = f32[1536,256]{1,0:T(8,128)} custom-call(s32[1,4]{1,0:T(1,128)} %bitcast.29, bf16[16,1536]{1,0:T(8,128)(2,1)} %bitcast.23, bf16[16,256]{1,0:T(8,128)(2,1)} %get-tuple-element.36.refs_2_, bf16[1536,256]{1,0:T(8,128)(2,1)} %bitcast.17, bf16[1536,256]{1,0:T(8,128)(2,1)} %bitcast.18, bf16[1536,256]{1,0:T(8,128)(2,1)} %get-tuple-element.37.refs_5_, ...), custom_call_target="tpu_custom_call" | custom-call | tf_op jit(solution)/shard_map/update/pallas_call | solution.py:58
  61.6 8.6 %solve.3 = (bf16[768,256]{1,0:T(8,128)(2,1)S(1)}, f32[512,256]{1,0:T(8,128)S(1)}, bf16[8,256]{1,0:T(8,128)(2,1)S(1)}, bf16[1536,256]{1,0:T(8,128)(2,1)}, bf16[25...) custom-call(s32[1,64]{1,0:T(1,128)} %bitcast.26, ...), custom_call_target="tpu_custom_call" | custom-call | tf_op jit(solution)/shard_map/solve/pallas_call | solution.py:58
  72.1 1.4 %pack.3 = (bf16[32,24,256]{2,1,0:T(8,128)(2,1)}, bf16[256,256]{1,0:T(8,128)(2,1)}) custom-call(f32[512,256]{1,0:T(8,128)S(1)} %get-tuple-element.43.refs_0_, bf16[768,256]{1,0:T(8,128)(2,1)S(1)} %collective-permute-done.11.refs_1_, bf16[8,256]{1,0:T(8,128)(2,1)S(1)} %get-tuple-element.45.refs_2_), custom_call_target="tpu_custom_call" | custom-call | tf_op jit(solution)/shard_map/pack/pallas_call | solution.py:58
  73.5 9.2 %all-to-all-start.2 = ((bf16[32,24,256]{2,1,0:T(8,128)(2,1)}), bf16[32,24,256]{2,1,0:T(8,128)(2,1)S(1)}, u32[]{:S(2)}, u32[]{:S(2)}) async-start(bf16[32,24,256]{2,1,0:T(8,128)(2,1)} %get-tuple-element.46), calls=%async_computation.2 | async-start | bytes 786432 | tf_op jit(solution)/shard_map/all_to_all | solution.py:45
  82.8 4.0 %collective-permute-start.12 = (bf16[256,256]{1,0:T(8,128)(2,1)S(1)}, bf16[256,256]{1,0:T(8,128)(2,1)S(1)}, u32[]{:S(2)}, u32[]{:S(2)}) collective-permute-start(bf16[256,256]{1,0:T(8,128)(2,1)S(1)} %copy-done.6), channel_id=1, source_target_pairs={{32,64},{96,128},{160,192},{64,32},{128,96},{192,160},{33,65},{97,... | collective-permute-start | bytes 393224 | tf_op jit(solution)/shard_map/ppermute | solution.py:29
  87.9 6.7 %all-to-all-done.2.refs_0_ = bf16[32,24,256]{2,1,0:T(8,128)(2,1)S(1)} async-done(((bf16[32,24,256]{2,1,0:T(8,128)(2,1)}), bf16[32,24,256]{2,1,0:T(8,128)(2,1)S(1)}, u32[]{:S(2)}, u32[]{:S(2)}) %all-to-all-start.2) | async-done | bytes 393248 | tf_op jit(solution)/shard_map/all_to_all | solution.py:45
  95.9 6.6 %all-to-all-start.3 = ((bf16[8,8,256]{2,1,0:T(8,128)(2,1)}), bf16[8,8,256]{2,1,0:T(8,128)(2,1)S(1)}, u32[]{:S(2)}, u32[]{:S(2)}) async-start(bf16[8,8,256]{2,1,0:T(8,128)(2,1)} %get-tuple-element.55), calls=%async_computation.3 | async-start | bytes 65536 | tf_op jit(solution)/shard_map/all_to_all | solution.py:45
  102.5 3.9 %update.3.base_hbm = f32[1536,256]{1,0:T(8,128)} custom-call(s32[1,4]{1,0:T(1,128)} %bitcast.30, bf16[16,1536]{1,0:T(8,128)(2,1)} %bitcast.24, bf16[16,256]{1,0:T(8,128)(2,1)} %get-tuple-element.48.refs_2_, bf16[1536,256]{1,0:T(8,128)(2,1)} %bitcast.19, f32[1536,256]{1,0:T(8,128)} %get-tuple-element.49.refs_4_, bf16[1536,256]{1,0:T(8,128)(2,1)} %get-tuple-element.50.refs_5_, ...), custom_call_target="tpu_custom_call" | custom-call | tf_op jit(solution)/shard_map/update/pallas_call | solution.py:58
  107.4 6.2 %final.1 = (f32[1536,256]{1,0:T(8,128)}, bf16[1536,256]{1,0:T(8,128)(2,1)}) custom-call(f32[1536,256]{1,0:T(8,128)} %update.3.base_hbm, bf16[8,8,256]{2,1,0:T(8,128)(2,1)S(1)} %all-to-all-done.3.shares_ref, bf16[8,1536]{1,0:T(8,128)(2,1)} %bitcast.22, bf16[1536,1536]{1,0:T(8,128)(2,1)} %bitcast.13), custom_call_target="tpu_custom_call" | custom-call | tf_op jit(solution)/shard_map/final/pallas_call | solution.py:58
  (40 shorter events, 11.0 us)
Async XLA Ops:
  8.7 4.6 %collective-permute-start = (bf16[768,256]{1,0:T(8,128)(2,1)S(1)}, bf16[768,256]{1,0:T(8,128)(2,1)S(1)}, u32[]{:S(2)}, u32[]{:S(2)}) collective-permute-start(bf16[768,256]{1,0:T(8,128)(2,1)S(1)} %get-tuple-element.31), channel_id=1, source_target_pairs={{0,32},{32,0},{1,33},{33,1},{2,34},{34,2},{3,35},{35,3},{4,36},{36... | collective-permute-start | bytes 1179656 | tf_op jit(solution)/shard_map/ppermute | solution.py:29
  14.8 33.8 %all-to-all-start = ((bf16[32,32,256]{2,1,0:T(8,128)(2,1)}), bf16[32,32,256]{2,1,0:T(8,128)(2,1)S(1)}, u32[]{:S(2)}, u32[]{:S(2)}) async-start(bf16[32,32,256]{2,1,0:T(8,128)(2,1)} %get-tuple-element.34), calls=%async_computation | async-start | bytes 1048576 | tf_op jit(solution)/shard_map/all_to_all | solution.py:45
  24.3 20.1 %copy-start.3 = (bf16[256,256]{1,0:T(8,128)(2,1)S(1)}, bf16[256,256]{1,0:T(8,128)(2,1)}, u32[]{:S(2)}) copy-start(bf16[256,256]{1,0:T(8,128)(2,1)} %get-tuple-element.39) | copy-start | bytes 393220
  24.3 23.4 %copy-start.2 = (bf16[256,256]{1,0:T(8,128)(2,1)S(1)}, bf16[256,256]{1,0:T(8,128)(2,1)}, u32[]{:S(2)}) copy-start(bf16[256,256]{1,0:T(8,128)(2,1)} %get-tuple-element.40) | copy-start | bytes 393220
  24.3 23.5 %copy-start.1 = (bf16[256,256]{1,0:T(8,128)(2,1)S(1)}, bf16[256,256]{1,0:T(8,128)(2,1)}, u32[]{:S(2)}) copy-start(bf16[256,256]{1,0:T(8,128)(2,1)} %get-tuple-element.41) | copy-start | bytes 393220
  24.3 3.7 %collective-permute-start.3 = (bf16[4,8,256]{2,1,0:T(8,128)(2,1)S(1)}, bf16[4,8,256]{2,1,0:T(8,128)(2,1)S(1)}, u32[]{:S(2)}, u32[]{:S(2)}) collective-permute-start(bf16[4,8,256]{2,1,0:T(8,128)(2,1)S(1)} %get-tuple-element.35), channel_id=1, source_target_pairs={{0,24},{8,0},{16,8},{24,16},{1,25},{9,1},{17,9},{25,17},{2,26},{10... | collective-permute-start | bytes 49160 | tf_op jit(solution)/shard_map/ppermute | solution.py:34
  26.9 4.1 %collective-permute-start.2 = (bf16[4,8,256]{2,1,0:T(8,128)(2,1)S(1)}, bf16[4,8,256]{2,1,0:T(8,128)(2,1)S(1)}, u32[]{:S(2)}, u32[]{:S(2)}) collective-permute-start(bf16[4,8,256]{2,1,0:T(8,128)(2,1)S(1)} %get-tuple-element.35), channel_id=1, source_target_pairs={{0,16},{8,24},{16,0},{24,8},{1,17},{9,25},{17,1},{25,9},{2,18},{10... | collective-permute-start | bytes 49160 | tf_op jit(solution)/shard_map/ppermute | solution.py:34
  27.4 3.8 %collective-permute-start.1 = (bf16[4,8,256]{2,1,0:T(8,128)(2,1)S(1)}, bf16[4,8,256]{2,1,0:T(8,128)(2,1)S(1)}, u32[]{:S(2)}, u32[]{:S(2)}) collective-permute-start(bf16[4,8,256]{2,1,0:T(8,128)(2,1)S(1)} %get-tuple-element.35), channel_id=1, source_target_pairs={{0,8},{8,16},{16,24},{24,0},{1,9},{9,17},{17,25},{25,1},{2,10},{10... | collective-permute-start | bytes 49160 | tf_op jit(solution)/shard_map/ppermute | solution.py:34
  33.3 4.2 %collective-permute-start.6 = (bf16[32,2048]{1,0:T(8,128)(2,1)S(1)}, bf16[32,2048]{1,0:T(8,128)(2,1)S(1)}, u32[]{:S(2)}, u32[]{:S(2)}) collective-permute-start(bf16[32,2048]{1,0:T(8,128)(2,1)S(1)} %rows.1), channel_id=1, source_target_pairs={{0,24},{8,0},{16,8},{24,16},{1,25},{9,1},{17,9},{25,17},{2,26},{10... | collective-permute-start | bytes 393224 | tf_op jit(solution)/shard_map/ppermute | solution.py:34
  33.9 5.6 %collective-permute-start.5 = (bf16[32,2048]{1,0:T(8,128)(2,1)S(1)}, bf16[32,2048]{1,0:T(8,128)(2,1)S(1)}, u32[]{:S(2)}, u32[]{:S(2)}) collective-permute-start(bf16[32,2048]{1,0:T(8,128)(2,1)S(1)} %rows.1), channel_id=1, source_target_pairs={{0,16},{8,24},{16,0},{24,8},{1,17},{9,25},{17,1},{25,9},{2,18},{10... | collective-permute-start | bytes 393224 | tf_op jit(solution)/shard_map/ppermute | solution.py:34
  35.0 6.1 %collective-permute-start.4 = (bf16[32,2048]{1,0:T(8,128)(2,1)S(1)}, bf16[32,2048]{1,0:T(8,128)(2,1)S(1)}, u32[]{:S(2)}, u32[]{:S(2)}) collective-permute-start(bf16[32,2048]{1,0:T(8,128)(2,1)S(1)} %rows.1), channel_id=1, source_target_pairs={{0,8},{8,16},{16,24},{24,0},{1,9},{9,17},{17,25},{25,1},{2,10},{10... | collective-permute-start | bytes 393224 | tf_op jit(solution)/shard_map/ppermute | solution.py:34
  41.1 7.4 %collective-permute-start.7 = (bf16[32,2048]{1,0:T(8,128)(2,1)S(1)}, bf16[32,2048]{1,0:T(8,128)(2,1)S(1)}, u32[]{:S(2)}, u32[]{:S(2)}) collective-permute-start(bf16[32,2048]{1,0:T(8,128)(2,1)S(1)} %add_add_fusion.refs_1_), channel_id=1, source_target_pairs={{0,32},{32,0},{1,33},{33,1},{2,34},{34,2},{3,35},{35,3},{4,36},{36... | collective-permute-start | bytes 393224 | tf_op jit(solution)/shard_map/ppermute | solution.py:29
  44.4 12.3 %collective-permute-start.8 = (bf16[256,256]{1,0:T(8,128)(2,1)S(1)}, bf16[256,256]{1,0:T(8,128)(2,1)S(1)}, u32[]{:S(2)}, u32[]{:S(2)}) collective-permute-start(bf16[256,256]{1,0:T(8,128)(2,1)S(1)} %copy-done.3), channel_id=1, source_target_pairs={{32,64},{96,128},{160,192},{64,32},{128,96},{192,160},{33,65},{97,... | collective-permute-start | bytes 393224 | tf_op jit(solution)/shard_map/ppermute | solution.py:29
  47.8 9.0 %collective-permute-start.9 = (bf16[256,256]{1,0:T(8,128)(2,1)S(1)}, bf16[256,256]{1,0:T(8,128)(2,1)S(1)}, u32[]{:S(2)}, u32[]{:S(2)}) collective-permute-start(bf16[256,256]{1,0:T(8,128)(2,1)S(1)} %copy-done.2), channel_id=1, source_target_pairs={{0,8},{16,24},{8,0},{24,16},{1,9},{17,25},{9,1},{25,17},{2,10},{18... | collective-permute-start | bytes 393224 | tf_op jit(solution)/shard_map/ppermute | solution.py:29
  47.9 8.8 %collective-permute-start.10 = (bf16[256,256]{1,0:T(8,128)(2,1)S(1)}, bf16[256,256]{1,0:T(8,128)(2,1)S(1)}, u32[]{:S(2)}, u32[]{:S(2)}) collective-permute-start(bf16[256,256]{1,0:T(8,128)(2,1)S(1)} %copy-done.1), channel_id=1, source_target_pairs={{8,16},{16,8},{9,17},{17,9},{10,18},{18,10},{11,19},{19,11},{12,20... | collective-permute-start | bytes 393224 | tf_op jit(solution)/shard_map/ppermute | solution.py:29
  50.6 11.1 %all-to-all-start.1 = ((bf16[8,8,256]{2,1,0:T(8,128)(2,1)}), bf16[8,8,256]{2,1,0:T(8,128)(2,1)S(1)}, u32[]{:S(2)}, u32[]{:S(2)}) async-start(bf16[8,8,256]{2,1,0:T(8,128)(2,1)} %get-tuple-element.42), calls=%async_computation.1 | async-start | bytes 65536 | tf_op jit(solution)/shard_map/all_to_all | solution.py:45
  70.3 16.9 %copy-start.4 = (bf16[256,256]{1,0:T(8,128)(2,1)S(1)}, bf16[256,256]{1,0:T(8,128)(2,1)}, u32[]{:S(2)}) copy-start(bf16[256,256]{1,0:T(8,128)(2,1)} %get-tuple-element.54) | copy-start | bytes 393220
  70.3 24.3 %copy-start = (bf16[2,32,256]{2,1,0:T(8,128)(2,1)S(1)}, bf16[2,32,256]{2,1,0:T(8,128)(2,1)}, u32[]{:S(2)}) copy-start(bf16[2,32,256]{2,1,0:T(8,128)(2,1)} %get-tuple-element.47.refs_1_) | copy-start | bytes 98308
  70.3 1.8 %collective-permute-start.11 = (bf16[768,256]{1,0:T(8,128)(2,1)S(1)}, bf16[768,256]{1,0:T(8,128)(2,1)S(1)}, u32[]{:S(2)}, u32[]{:S(2)}) collective-permute-start(bf16[768,256]{1,0:T(8,128)(2,1)S(1)} %get-tuple-element.44), channel_id=1, source_target_pairs={{0,32},{32,0},{1,33},{33,1},{2,34},{34,2},{3,35},{35,3},{4,36},{36... | collective-permute-start | bytes 1179656 | tf_op jit(solution)/shard_map/ppermute | solution.py:29
  73.5 21.0 %all-to-all-start.2 = ((bf16[32,24,256]{2,1,0:T(8,128)(2,1)}), bf16[32,24,256]{2,1,0:T(8,128)(2,1)S(1)}, u32[]{:S(2)}, u32[]{:S(2)}) async-start(bf16[32,24,256]{2,1,0:T(8,128)(2,1)} %get-tuple-element.46), calls=%async_computation.2 | async-start | bytes 786432 | tf_op jit(solution)/shard_map/all_to_all | solution.py:45
  82.8 19.7 %collective-permute-start.12 = (bf16[256,256]{1,0:T(8,128)(2,1)S(1)}, bf16[256,256]{1,0:T(8,128)(2,1)S(1)}, u32[]{:S(2)}, u32[]{:S(2)}) collective-permute-start(bf16[256,256]{1,0:T(8,128)(2,1)S(1)} %copy-done.6), channel_id=1, source_target_pairs={{32,64},{96,128},{160,192},{64,32},{128,96},{192,160},{33,65},{97,... | collective-permute-start | bytes 393224 | tf_op jit(solution)/shard_map/ppermute | solution.py:29
  86.7 15.7 %collective-permute-start.13 = (bf16[256,256]{1,0:T(8,128)(2,1)S(1)}, bf16[256,256]{1,0:T(8,128)(2,1)S(1)}, u32[]{:S(2)}, u32[]{:S(2)}) collective-permute-start(bf16[256,256]{1,0:T(8,128)(2,1)S(1)} %copy-done.5), channel_id=1, source_target_pairs={{0,8},{16,24},{8,0},{24,16},{1,9},{17,25},{9,1},{25,17},{2,10},{18... | collective-permute-start | bytes 393224 | tf_op jit(solution)/shard_map/ppermute | solution.py:29
  87.2 15.3 %collective-permute-start.14 = (bf16[256,256]{1,0:T(8,128)(2,1)S(1)}, bf16[256,256]{1,0:T(8,128)(2,1)S(1)}, u32[]{:S(2)}, u32[]{:S(2)}) collective-permute-start(bf16[256,256]{1,0:T(8,128)(2,1)S(1)} %copy-done.4), channel_id=1, source_target_pairs={{8,16},{16,8},{9,17},{17,9},{10,18},{18,10},{11,19},{19,11},{12,20... | collective-permute-start | bytes 393224 | tf_op jit(solution)/shard_map/ppermute | solution.py:29
  95.9 11.5 %all-to-all-start.3 = ((bf16[8,8,256]{2,1,0:T(8,128)(2,1)}), bf16[8,8,256]{2,1,0:T(8,128)(2,1)S(1)}, u32[]{:S(2)}, u32[]{:S(2)}) async-start(bf16[8,8,256]{2,1,0:T(8,128)(2,1)} %get-tuple-element.55), calls=%async_computation.3 | async-start | bytes 65536 | tf_op jit(solution)/shard_map/all_to_all | solution.py:45
  (2 other events, 29.0 us)
